TPU v7x, 256 devices: a whole 4x4x8 slice. The times are simulated.
256 devices in a mesh: gx: 16 (over z, core), gy: 8 (over x_hi, y), gz: 2 (over x_lo).
Axes of the slice: x: 4 (x_hi: 2, x_lo: 2; x = x_hi * 2 + x_lo), y: 4, z: 8, core: 2. Of those that a mesh axis runs over, the one named last changes fastest.
Arguments:
- load_current: float32 [1536, 8192], P('gy', 'gx'), may hold values from 0 to 90
- sink_mask: int32 [1536, 8192], P('gy', 'gx'), may hold values 0 or 1
- pad_mask: int32 [1536, 8192], P('gy', 'gx'), may hold values from 0 to 1, as said below
- plane_class: int32 [4, 1536, 8192], P('gz', 'gy', 'gx'), may hold values from 0 to 7
- via_class: int32 [4, 1536, 8192], P('gz', 'gy', 'gx'), may hold values from 0 to 7
- plane_table: float32 [4, 8], P('gz'), may hold values from 0.25 to 4
- via_table: float32 [4, 8], P('gz'), may hold values from 0.25 to 4
Outputs:
- voltage: float32 [4, 1536, 8192], P('gz', 'gy', 'gx')
- residual: float32 [4, 1536, 8192], P('gz', 'gy', 'gx')
Inputs may be any that keep to these rules, and one draw needn't show every extreme that they name: `pad_mask`: exactly one pad in each aligned 8 x 8 tile of nodes.
All inputs are finite; a program needn't handle non-finite values. No bound on the sum of `sink_mask` on one device may be relied on, other than what follows from the above.
Results may differ from a plain program's by a relative error of at most 0.00012.
Values sent between devices are 32-bit elements; how exact they have to be, the bound alone decides.
A program may use at most 64 MiB of HBM per device.

v0:
```python
import jax
import jax.numpy as jnp
from jax import lax
from jax.sharding import Mesh
from jax.sharding import PartitionSpec as P

ITERS = 3
GX = ("gx_0", "gx_1")
GY = ("gy_0", "gy_1")
GX_GY_GZ = ("gx_0", "gx_1", "gy_0", "gy_1", "gz")


PAD_CONDUCTANCE = 20.0


def padded(array, sides, width):
    edges = {}
    for axis, dim in sides:
        peers, length = (lax.axis_size(axis), array.shape[dim])
        up = [(i, (i + 1) % peers) for i in range(peers)]
        last = lax.slice_in_dim(array, length - width, length, axis=dim)
        leading = lax.slice_in_dim(array, 0, width, axis=dim)
        edges[dim] = (
            lax.ppermute(last, axis, up),
            lax.ppermute(leading, axis, [(b, a) for a, b in up]),
        )
    done = []
    for _, dim in sides:
        low, high = edges[dim]
        around = [(width, width) if d in done else (0, 0) for d in range(array.ndim)]
        array = jnp.concatenate([jnp.pad(low, around), array, jnp.pad(high, around)], axis=dim)
        done.append(dim)
    return array


def padded_2(block, sides, width):
    for axis, dim in sides:
        count = lax.axis_size(axis)
        forward = [(i, i + 1) for i in range(count - 1)]
        backward = [(target, source) for source, target in forward]
        low = lax.ppermute(
            lax.slice_in_dim(block, block.shape[dim] - width, None, axis=dim), axis, forward
        )
        high = lax.ppermute(lax.slice_in_dim(block, 0, width, axis=dim), axis, backward)
        block = jnp.concatenate([low, block, high], axis=dim)
    return block


def by_axis(array, axes):
    for axis in axes:
        array = lax.psum(array, axis)
    return array


def lookup(classes, table):
    summed = jnp.zeros(classes.shape, jnp.float32)
    for level in range(table.shape[1]):
        summed = summed + jnp.where(
            classes == level, table[:, level][:, None, None], jnp.float32(0.0)
        )
    return summed


def harmonic(first, second):
    return 2.0 * first * second / (first + second)


def factor(diagonal, up_edge):
    inverses = []
    factors = []
    for level in range(diagonal.shape[0]):
        pivots = diagonal[level]
        if level > 0:
            pivots = pivots + up_edge[level - 1] * factors[level - 1]
        inverse = 1.0 / pivots
        inverses.append(inverse)
        factors.append(-up_edge[level] * inverse)
    return (jnp.stack(inverses), jnp.stack(factors))


def solve_block(inverses, factors, up_edge, source_term):
    forward = []
    for level in range(source_term.shape[0]):
        entries = source_term[level]
        if level > 0:
            entries = entries + up_edge[level - 1] * forward[level - 1]
        forward.append(entries * inverses[level])
    result = [forward[-1]]
    level = 0
    result.insert(0, forward[level] - factors[level] * result[0])
    return jnp.stack(result)


def plane_extend(field):
    return padded(field, ((GX, 2), (GY, 1)), 1)


def layer_extend(field):
    return padded_2(field, (("gz", 0),), 1)


def merged_sums(residual, precond, image_field):
    return (
        by_axis(jnp.sum(residual * precond), GX_GY_GZ),
        by_axis(jnp.sum(image_field * precond), GX_GY_GZ),
    )


def shards(load_current, sink_mask, pad_mask, plane_class, via_class, plane_table, via_table):
    n_layers, n_rows, n_cols = plane_class.shape
    g_plane = lookup(plane_class, plane_table)
    g_via = lookup(via_class, via_table)
    plane_ext = plane_extend(g_plane)
    middle = plane_ext[:, 1:-1, :]
    across = harmonic(middle[:, :, :-1], middle[:, :, 1:])
    east_edge = across[:, :, 1:]
    west_edge = across[:, :, :-1]
    column = plane_ext[:, :, 1:-1]
    along_rows = harmonic(column[:, :-1], column[:, 1:])
    north_edge = along_rows[:, 1:]
    south_edge = along_rows[:, :-1]
    via_ext = layer_extend(g_via)
    vertical = harmonic(via_ext[:-1], via_ext[1:])
    up_edge = vertical[1:]
    down_edge = vertical[:-1]
    group_index = lax.axis_index("gz")
    is_top = group_index == lax.axis_size("gz") - 1
    is_bottom = group_index == 0
    pad_plane = jnp.where(is_top, PAD_CONDUCTANCE * pad_mask.astype(jnp.float32), jnp.float32(0.0))
    pad_layer = jnp.concatenate(
        [jnp.zeros((n_layers - 1, n_rows, n_cols), jnp.float32), pad_plane[None]], 0
    )
    diagonal = east_edge + west_edge + north_edge + south_edge + up_edge + down_edge + pad_layer
    inverses, factors = factor(diagonal, up_edge)

    def precondition(residual):
        return solve_block(inverses, factors, up_edge, residual)

    def operate(field):
        inner = plane_extend(field)
        layer_ext = layer_extend(field)
        above_field = layer_ext[2:]
        below_field = layer_ext[:-2]
        return (
            diagonal * field
            - east_edge * inner[:, 1:-1, 2:]
            - west_edge * inner[:, 1:-1, :-2]
            - north_edge * inner[:, 2:, 1:-1]
            - south_edge * inner[:, :-2, 1:-1]
            - up_edge * above_field
            - down_edge * below_field
        )

    source = jnp.where(is_bottom, sink_mask.astype(jnp.float32) * load_current, jnp.float32(0.0))
    right_side = jnp.concatenate(
        [source[None], jnp.zeros((n_layers - 1, n_rows, n_cols), jnp.float32)], 0
    )
    voltage = jnp.zeros((n_layers, n_rows, n_cols), jnp.float32)
    residual = right_side
    precond = precondition(residual)
    image_field = operate(precond)
    weight_now, curvature = merged_sums(residual, precond, image_field)
    step_size = weight_now / curvature
    direction = precond
    image_dir = image_field
    for iteration in range(ITERS):
        voltage = voltage + step_size * direction
        residual = residual - step_size * image_dir
        if iteration + 1 < ITERS:
            precond = precondition(residual)
            image_field = operate(precond)
            weight_next, curvature = merged_sums(residual, precond, image_field)
            momentum = weight_next / weight_now
            step_size = weight_next / (curvature - momentum * weight_next / step_size)
            direction = precond + momentum * direction
            image_dir = image_field + momentum * image_dir
            weight_now = weight_next
    return (voltage, residual)


def solution(mesh):
    split = Mesh(
        mesh.devices.reshape(8, 2, 2, 4, mesh.shape["gz"]), ("gx_0", "gx_1", "gy_0", "gy_1", "gz")
    )
    placed = (
        P(GY, GX),
        P(GY, GX),
        P(GY, GX),
        P("gz", GY, GX),
        P("gz", GY, GX),
        P("gz", None),
        P("gz", None),
    )
    return jax.shard_map(
        shards,
        mesh=split,
        in_specs=placed,
        out_specs=(P("gz", GY, GX), P("gz", GY, GX)),
        check_vma=False,
    )
```

profile of v0, /device:TPU:1, one launch (start us, length us, event | category | flops | bytes accessed | tf_op | source)
XLA Modules:
  0.0 243.1 jit_solution(2650260789971561995)
XLA Ops:
  16.5 4.5 %collective-permute-start.3 = (f32[2,1,512]{2,1,0:T(1,128)S(1)}, f32[2,1,512]{2,1,0:T(1,128)S(1)}, u32[]{:S(2)}, u32[]{:S(2)}) collective-permute-start(f32[2,1,512]{2,1,0:T(1,128)S(1)} %get-tuple-element.76), channel_id=1, source_target_pairs={{2,0},{4,2},{6,4},{8,6},{10,8},{12,10},{14,12},{0,14},{3,1},{5,3},... | collective-permute-start | bytes 12296 | tf_op jit(solution)/shard_map/ppermute | solution.py:25
  28.9 4.0 %collective-permute-start.11 = (f32[1,192,512]{2,1,0:T(8,128)S(1)}, f32[1,192,512]{2,1,0:T(8,128)S(1)}, u32[]{:S(2)}, u32[]{:S(2)}) collective-permute-start(f32[1,192,512]{2,1,0:T(8,128)S(1)} %get-tuple-element.61), channel_id=1, source_target_pairs={{0,1},{2,3},{4,5},{6,7},{8,9},{10,11},{12,13},{14,15},{16,17},{18,... | collective-permute-start | bytes 1179656 | tf_op jit(solution)/shard_map/ppermute | solution.py:41
  32.9 5.3 %collective-permute-start.8 = (f32[2,1,512]{2,1,0:T(1,128)S(1)}, f32[2,1,512]{2,1,0:T(1,128)S(1)}, u32[]{:S(2)}, u32[]{:S(2)}) collective-permute-start(f32[2,1,512]{2,1,0:T(1,128)S(1)} %get-tuple-element.71), channel_id=1, source_target_pairs={{2,0},{4,2},{6,4},{8,6},{10,8},{12,10},{14,12},{0,14},{3,1},{5,3},... | collective-permute-start | bytes 12296 | tf_op jit(solution)/shard_map/ppermute | solution.py:25
  38.3 6.7 %collective-permute-start.7 = (f32[2,192,1]{2,1,0:T(8,128)S(1)}, f32[2,192,1]{2,1,0:T(8,128)S(1)}, u32[]{:S(2)}, u32[]{:S(2)}) collective-permute-start(f32[2,192,1]{2,1,0:T(8,128)S(1)} %get-tuple-element.73), channel_id=1, source_target_pairs={{0,16},{16,32},{32,48},{48,64},{64,80},{80,96},{96,112},{112,128},... | collective-permute-start | bytes 4616 | tf_op jit(solution)/shard_map/ppermute | solution.py:24
  56.6 15.4 %all-reduce.12 = (f32[]{:T(128)}, f32[]{:T(128)}) all-reduce(f32[]{:T(128)} %get-tuple-element.7, f32[]{:T(128)} %get-tuple-element.6), channel_id=1, replica_groups=mesh['gx_0'=8,'gx_1'=2,'gy_0'=2,'gy_1'=4,'gz'=2] {'gx_0'}, use_global_device_ids=true, to_apply=%region_1.2 | all-reduce | flops 2 | bytes 16 | tf_op jit(solution)/shard_map/psum | solution.py:51
  71.9 4.9 %all-reduce.24 = (f32[]{:T(128)}, f32[]{:T(128)}) all-reduce(f32[]{:T(128)} %get-tuple-element.28, f32[]{:T(128)} %get-tuple-element.29), channel_id=1, replica_groups=mesh['gx_0'=8,'gx_1'=2,'gy_0'=2,'gy_1'=4,'gz'=2] {'gx_1'}, use_global_device_ids=true, to_apply=%region_2.3 | all-reduce | flops 2 | bytes 16 | tf_op jit(solution)/shard_map/psum | solution.py:51
  76.8 6.0 %all-reduce.21 = (f32[]{:T(128)}, f32[]{:T(128)}) all-reduce(f32[]{:T(128)} %get-tuple-element.52, f32[]{:T(128)} %get-tuple-element.53), channel_id=1, replica_groups=mesh['gx_0'=8,'gx_1'=2,'gy_0'=2,'gy_1'=4,'gz'=2] {'gy_0'}, use_global_device_ids=true, to_apply=%region_3.4 | all-reduce | flops 2 | bytes 16 | tf_op jit(solution)/shard_map/psum | solution.py:51
  82.8 10.5 %all-reduce.15 = (f32[]{:T(128)}, f32[]{:T(128)}) all-reduce(f32[]{:T(128)} %get-tuple-element.46, f32[]{:T(128)} %get-tuple-element.47), channel_id=1, replica_groups=mesh['gx_0'=8,'gx_1'=2,'gy_0'=2,'gy_1'=4,'gz'=2] {'gy_1'}, use_global_device_ids=true, to_apply=%region_4.5 | all-reduce | flops 2 | bytes 16 | tf_op jit(solution)/shard_map/psum | solution.py:51
  93.3 4.4 %all-reduce.18 = (f32[]{:T(128)}, f32[]{:T(128)}) all-reduce(f32[]{:T(128)} %get-tuple-element.34, f32[]{:T(128)} %get-tuple-element.35), channel_id=1, replica_groups=mesh['gx_0'=8,'gx_1'=2,'gy_0'=2,'gy_1'=4,'gz'=2] {'gz'}, use_global_device_ids=true, to_apply=%region_5.6 | all-reduce | flops 2 | bytes 16 | tf_op jit(solution)/shard_map/psum | solution.py:51
  102.1 4.0 %collective-permute-start.17 = (f32[1,192,512]{2,1,0:T(8,128)S(1)}, f32[1,192,512]{2,1,0:T(8,128)S(1)}, u32[]{:S(2)}, u32[]{:S(2)}) collective-permute-start(f32[1,192,512]{2,1,0:T(8,128)S(1)} %get-tuple-element.59), channel_id=1, source_target_pairs={{0,1},{2,3},{4,5},{6,7},{8,9},{10,11},{12,13},{14,15},{16,17},{18,... | collective-permute-start | bytes 1179656 | tf_op jit(solution)/shard_map/ppermute | solution.py:41
  107.9 5.8 %collective-permute-start.13 = (f32[2,192,1]{2,1,0:T(8,128)S(1)}, f32[2,192,1]{2,1,0:T(8,128)S(1)}, u32[]{:S(2)}, u32[]{:S(2)}) collective-permute-start(f32[2,192,1]{2,1,0:T(8,128)S(1)} %get-tuple-element.69), channel_id=1, source_target_pairs={{0,16},{16,32},{32,48},{48,64},{64,80},{80,96},{96,112},{112,128},... | collective-permute-start | bytes 4616 | tf_op jit(solution)/shard_map/ppermute | solution.py:24
  125.4 15.1 %all-reduce.11 = (f32[]{:T(128)}, f32[]{:T(128)}) all-reduce(f32[]{:T(128)} %get-tuple-element.5, f32[]{:T(128)} %get-tuple-element.4), channel_id=1, replica_groups=mesh['gx_0'=8,'gx_1'=2,'gy_0'=2,'gy_1'=4,'gz'=2] {'gx_0'}, use_global_device_ids=true, to_apply=%region_13.14 | all-reduce | flops 2 | bytes 16 | tf_op jit(solution)/shard_map/psum | solution.py:51
  140.5 4.1 %all-reduce.23 = (f32[]{:T(128)}, f32[]{:T(128)}) all-reduce(f32[]{:T(128)} %get-tuple-element.26, f32[]{:T(128)} %get-tuple-element.27), channel_id=1, replica_groups=mesh['gx_0'=8,'gx_1'=2,'gy_0'=2,'gy_1'=4,'gz'=2] {'gx_1'}, use_global_device_ids=true, to_apply=%region_14.15 | all-reduce | flops 2 | bytes 16 | tf_op jit(solution)/shard_map/psum | solution.py:51
  144.6 5.9 %all-reduce.20 = (f32[]{:T(128)}, f32[]{:T(128)}) all-reduce(f32[]{:T(128)} %get-tuple-element.50, f32[]{:T(128)} %get-tuple-element.51), channel_id=1, replica_groups=mesh['gx_0'=8,'gx_1'=2,'gy_0'=2,'gy_1'=4,'gz'=2] {'gy_0'}, use_global_device_ids=true, to_apply=%region_15.16 | all-reduce | flops 2 | bytes 16 | tf_op jit(solution)/shard_map/psum | solution.py:51
  150.5 9.8 %all-reduce.14 = (f32[]{:T(128)}, f32[]{:T(128)}) all-reduce(f32[]{:T(128)} %get-tuple-element.44, f32[]{:T(128)} %get-tuple-element.45), channel_id=1, replica_groups=mesh['gx_0'=8,'gx_1'=2,'gy_0'=2,'gy_1'=4,'gz'=2] {'gy_1'}, use_global_device_ids=true, to_apply=%region_16.17 | all-reduce | flops 2 | bytes 16 | tf_op jit(solution)/shard_map/psum | solution.py:51
  160.3 4.4 %all-reduce.17 = (f32[]{:T(128)}, f32[]{:T(128)}) all-reduce(f32[]{:T(128)} %get-tuple-element.32, f32[]{:T(128)} %get-tuple-element.33), channel_id=1, replica_groups=mesh['gx_0'=8,'gx_1'=2,'gy_0'=2,'gy_1'=4,'gz'=2] {'gz'}, use_global_device_ids=true, to_apply=%region_17.18 | all-reduce | flops 2 | bytes 16 | tf_op jit(solution)/shard_map/psum | solution.py:51
  172.6 4.0 %collective-permute-start.23 = (f32[1,192,512]{2,1,0:T(8,128)S(1)}, f32[1,192,512]{2,1,0:T(8,128)S(1)}, u32[]{:S(2)}, u32[]{:S(2)}) collective-permute-start(f32[1,192,512]{2,1,0:T(8,128)S(1)} %get-tuple-element.56), channel_id=1, source_target_pairs={{0,1},{2,3},{4,5},{6,7},{8,9},{10,11},{12,13},{14,15},{16,17},{18,... | collective-permute-start | bytes 1179656 | tf_op jit(solution)/shard_map/ppermute | solution.py:41
  178.3 7.0 %collective-permute-start.19 = (f32[2,192,1]{2,1,0:T(8,128)S(1)}, f32[2,192,1]{2,1,0:T(8,128)S(1)}, u32[]{:S(2)}, u32[]{:S(2)}) collective-permute-start(f32[2,192,1]{2,1,0:T(8,128)S(1)} %get-tuple-element.65), channel_id=1, source_target_pairs={{0,16},{16,32},{32,48},{48,64},{64,80},{80,96},{96,112},{112,128},... | collective-permute-start | bytes 4616 | tf_op jit(solution)/shard_map/ppermute | solution.py:24
  197.0 13.9 %all-reduce.10 = (f32[]{:T(128)}, f32[]{:T(128)}) all-reduce(f32[]{:T(128)} %get-tuple-element.3, f32[]{:T(128)} %get-tuple-element.2), channel_id=1, replica_groups=mesh['gx_0'=8,'gx_1'=2,'gy_0'=2,'gy_1'=4,'gz'=2] {'gx_0'}, use_global_device_ids=true, to_apply=%region_25.26 | all-reduce | flops 2 | bytes 16 | tf_op jit(solution)/shard_map/psum | solution.py:51
  210.8 4.0 %all-reduce.22 = (f32[]{:T(128)}, f32[]{:T(128)}) all-reduce(f32[]{:T(128)} %get-tuple-element.24, f32[]{:T(128)} %get-tuple-element.25), channel_id=1, replica_groups=mesh['gx_0'=8,'gx_1'=2,'gy_0'=2,'gy_1'=4,'gz'=2] {'gx_1'}, use_global_device_ids=true, to_apply=%region_26.27 | all-reduce | flops 2 | bytes 16 | tf_op jit(solution)/shard_map/psum | solution.py:51
  214.8 5.9 %all-reduce.19 = (f32[]{:T(128)}, f32[]{:T(128)}) all-reduce(f32[]{:T(128)} %get-tuple-element.48, f32[]{:T(128)} %get-tuple-element.49), channel_id=1, replica_groups=mesh['gx_0'=8,'gx_1'=2,'gy_0'=2,'gy_1'=4,'gz'=2] {'gy_0'}, use_global_device_ids=true, to_apply=%region_27.28 | all-reduce | flops 2 | bytes 16 | tf_op jit(solution)/shard_map/psum | solution.py:51
  220.8 9.7 %all-reduce.13 = (f32[]{:T(128)}, f32[]{:T(128)}) all-reduce(f32[]{:T(128)} %get-tuple-element.42, f32[]{:T(128)} %get-tuple-element.43), channel_id=1, replica_groups=mesh['gx_0'=8,'gx_1'=2,'gy_0'=2,'gy_1'=4,'gz'=2] {'gy_1'}, use_global_device_ids=true, to_apply=%region_28.29 | all-reduce | flops 2 | bytes 16 | tf_op jit(solution)/shard_map/psum | solution.py:51
  230.5 4.4 %all-reduce.16 = (f32[]{:T(128)}, f32[]{:T(128)}) all-reduce(f32[]{:T(128)} %get-tuple-element.30, f32[]{:T(128)} %get-tuple-element.31), channel_id=1, replica_groups=mesh['gx_0'=8,'gx_1'=2,'gy_0'=2,'gy_1'=4,'gz'=2] {'gz'}, use_global_device_ids=true, to_apply=%region_29.30 | all-reduce | flops 2 | bytes 16 | tf_op jit(solution)/shard_map/psum | solution.py:51
  238.7 4.4 %multiply_subtract_fusion = (f32[2,192,512]{2,1,0:T(8,128)}, f32[2,192,512]{2,1,0:T(8,128)}) fusion(f32[2,192,512]{2,1,0:T(8,128)} %copy-done.4, f32[2,192,512]{2,1,0:T(8,128)} %get-tuple-element.54, f32[]{:T(128)S(6)} %div.60, f32[]{:T(128)S(6)} %div.62, f32[2,192,512]{2,1,0:T(8,128)} %get-tuple-element.57, f32[2,192,512]{2,1,0:T(8,128)} %get-tuple-element.60, ...), kind=kLoop, calls=%fused_computation.127 | loop fusion | flops 3538944 | bytes 7077908 | tf_op jit(solution)/shard_map/sub | solution.py:168
  (115 shorter events, 68.2 us)
Async XLA Ops:
  3.8 17.5 %collective-permute-start.2 = (f32[2,1,512]{2,1,0:T(1,128)S(1)}, f32[2,1,512]{2,1,0:T(1,128)S(1)}, u32[]{:S(2)}, u32[]{:S(2)}) collective-permute-start(f32[2,1,512]{2,1,0:T(1,128)S(1)} %get-tuple-element.75), channel_id=1, source_target_pairs={{0,2},{2,4},{4,6},{6,8},{8,10},{10,12},{12,14},{14,0},{1,3},{3,5},... | collective-permute-start | bytes 12296 | tf_op jit(solution)/shard_map/ppermute | solution.py:24
  6.8 9.7 %collective-permute-start = (f32[2,192,1]{2,1,0:T(8,128)}, f32[2,192,1]{2,1,0:T(8,128)S(1)}, u32[]{:S(2)}, u32[]{:S(2)}) collective-permute-start(f32[2,192,1]{2,1,0:T(8,128)} %get-tuple-element.77), channel_id=1, source_target_pairs={{0,16},{16,32},{32,48},{48,64},{64,80},{80,96},{96,112},{112,128},... | collective-permute-start | bytes 4616 | tf_op jit(solution)/shard_map/ppermute | solution.py:24
  9.3 11.7 %collective-permute-start.1 = (f32[2,192,1]{2,1,0:T(8,128)S(1)}, f32[2,192,1]{2,1,0:T(8,128)S(1)}, u32[]{:S(2)}, u32[]{:S(2)}) collective-permute-start(f32[2,192,1]{2,1,0:T(8,128)S(1)} %get-tuple-element.78), channel_id=1, source_target_pairs={{16,0},{32,16},{48,32},{64,48},{80,64},{96,80},{112,96},{128,112},... | collective-permute-start | bytes 4616 | tf_op jit(solution)/shard_map/ppermute | solution.py:25
  11.2 11.8 %collective-permute-start.4 = (f32[1,192,512]{2,1,0:T(8,128)}, f32[1,192,512]{2,1,0:T(8,128)}, u32[]{:S(2)}, u32[]{:S(2)}) collective-permute-start(f32[1,192,512]{2,1,0:T(8,128)} %get-tuple-element.79), channel_id=1, source_target_pairs={{0,1},{2,3},{4,5},{6,7},{8,9},{10,11},{12,13},{14,15},{16,17},{18,... | collective-permute-start | bytes 1179656 | tf_op jit(solution)/shard_map/ppermute | solution.py:41
  15.0 8.8 %collective-permute-start.5 = (f32[1,192,512]{2,1,0:T(8,128)}, f32[1,192,512]{2,1,0:T(8,128)}, u32[]{:S(2)}, u32[]{:S(2)}) collective-permute-start(f32[1,192,512]{2,1,0:T(8,128)} %get-tuple-element.80), channel_id=1, source_target_pairs={{1,0},{3,2},{5,4},{7,6},{9,8},{11,10},{13,12},{15,14},{17,16},{19,... | collective-permute-start | bytes 1179656 | tf_op jit(solution)/shard_map/ppermute | solution.py:44
  16.5 5.2 %collective-permute-start.3 = (f32[2,1,512]{2,1,0:T(1,128)S(1)}, f32[2,1,512]{2,1,0:T(1,128)S(1)}, u32[]{:S(2)}, u32[]{:S(2)}) collective-permute-start(f32[2,1,512]{2,1,0:T(1,128)S(1)} %get-tuple-element.76), channel_id=1, source_target_pairs={{2,0},{4,2},{6,4},{8,6},{10,8},{12,10},{14,12},{0,14},{3,1},{5,3},... | collective-permute-start | bytes 12296 | tf_op jit(solution)/shard_map/ppermute | solution.py:25
  27.4 26.0 %collective-permute-start.10 = (f32[1,192,512]{2,1,0:T(8,128)S(1)}, f32[1,192,512]{2,1,0:T(8,128)S(1)}, u32[]{:S(2)}, u32[]{:S(2)}) collective-permute-start(f32[1,192,512]{2,1,0:T(8,128)S(1)} %subtract_bitcast_fusion), channel_id=1, source_target_pairs={{1,0},{3,2},{5,4},{7,6},{9,8},{11,10},{13,12},{15,14},{17,16},{19,... | collective-permute-start | bytes 1179656 | tf_op jit(solution)/shard_map/ppermute | solution.py:44
  28.9 24.6 %collective-permute-start.11 = (f32[1,192,512]{2,1,0:T(8,128)S(1)}, f32[1,192,512]{2,1,0:T(8,128)S(1)}, u32[]{:S(2)}, u32[]{:S(2)}) collective-permute-start(f32[1,192,512]{2,1,0:T(8,128)S(1)} %get-tuple-element.61), channel_id=1, source_target_pairs={{0,1},{2,3},{4,5},{6,7},{8,9},{10,11},{12,13},{14,15},{16,17},{18,... | collective-permute-start | bytes 1179656 | tf_op jit(solution)/shard_map/ppermute | solution.py:41
  32.9 20.5 %collective-permute-start.8 = (f32[2,1,512]{2,1,0:T(1,128)S(1)}, f32[2,1,512]{2,1,0:T(1,128)S(1)}, u32[]{:S(2)}, u32[]{:S(2)}) collective-permute-start(f32[2,1,512]{2,1,0:T(1,128)S(1)} %get-tuple-element.71), channel_id=1, source_target_pairs={{2,0},{4,2},{6,4},{8,6},{10,8},{12,10},{14,12},{0,14},{3,1},{5,3},... | collective-permute-start | bytes 12296 | tf_op jit(solution)/shard_map/ppermute | solution.py:25
  38.2 15.3 %collective-permute-start.9 = (f32[2,1,512]{2,1,0:T(1,128)S(1)}, f32[2,1,512]{2,1,0:T(1,128)S(1)}, u32[]{:S(2)}, u32[]{:S(2)}) collective-permute-start(f32[2,1,512]{2,1,0:T(1,128)S(1)} %get-tuple-element.72), channel_id=1, source_target_pairs={{0,2},{2,4},{4,6},{6,8},{8,10},{10,12},{12,14},{14,0},{1,3},{3,5},... | collective-permute-start | bytes 12296 | tf_op jit(solution)/shard_map/ppermute | solution.py:24
  38.3 9.3 %collective-permute-start.7 = (f32[2,192,1]{2,1,0:T(8,128)S(1)}, f32[2,192,1]{2,1,0:T(8,128)S(1)}, u32[]{:S(2)}, u32[]{:S(2)}) collective-permute-start(f32[2,192,1]{2,1,0:T(8,128)S(1)} %get-tuple-element.73), channel_id=1, source_target_pairs={{0,16},{16,32},{32,48},{48,64},{64,80},{80,96},{96,112},{112,128},... | collective-permute-start | bytes 4616 | tf_op jit(solution)/shard_map/ppermute | solution.py:24
  47.6 5.8 %collective-permute-start.6 = (f32[2,192,1]{2,1,0:T(8,128)S(1)}, f32[2,192,1]{2,1,0:T(8,128)S(1)}, u32[]{:S(2)}, u32[]{:S(2)}) collective-permute-start(f32[2,192,1]{2,1,0:T(8,128)S(1)} %get-tuple-element.74), channel_id=1, source_target_pairs={{16,0},{32,16},{48,32},{64,48},{80,64},{96,80},{112,96},{128,112},... | collective-permute-start | bytes 4616 | tf_op jit(solution)/shard_map/ppermute | solution.py:25
  100.7 21.4 %collective-permute-start.16 = (f32[1,192,512]{2,1,0:T(8,128)S(1)}, f32[1,192,512]{2,1,0:T(8,128)S(1)}, u32[]{:S(2)}, u32[]{:S(2)}) collective-permute-start(f32[1,192,512]{2,1,0:T(8,128)S(1)} %get-tuple-element.58), channel_id=1, source_target_pairs={{1,0},{3,2},{5,4},{7,6},{9,8},{11,10},{13,12},{15,14},{17,16},{19,... | collective-permute-start | bytes 1179656 | tf_op jit(solution)/shard_map/ppermute | solution.py:44
  102.1 20.0 %collective-permute-start.17 = (f32[1,192,512]{2,1,0:T(8,128)S(1)}, f32[1,192,512]{2,1,0:T(8,128)S(1)}, u32[]{:S(2)}, u32[]{:S(2)}) collective-permute-start(f32[1,192,512]{2,1,0:T(8,128)S(1)} %get-tuple-element.59), channel_id=1, source_target_pairs={{0,1},{2,3},{4,5},{6,7},{8,9},{10,11},{12,13},{14,15},{16,17},{18,... | collective-permute-start | bytes 1179656 | tf_op jit(solution)/shard_map/ppermute | solution.py:41
  106.2 15.9 %collective-permute-start.14 = (f32[2,1,512]{2,1,0:T(1,128)S(1)}, f32[2,1,512]{2,1,0:T(1,128)S(1)}, u32[]{:S(2)}, u32[]{:S(2)}) collective-permute-start(f32[2,1,512]{2,1,0:T(1,128)S(1)} %get-tuple-element.67), channel_id=1, source_target_pairs={{2,0},{4,2},{6,4},{8,6},{10,8},{12,10},{14,12},{0,14},{3,1},{5,3},... | collective-permute-start | bytes 12296 | tf_op jit(solution)/shard_map/ppermute | solution.py:25
  107.5 14.6 %collective-permute-start.15 = (f32[2,1,512]{2,1,0:T(1,128)S(1)}, f32[2,1,512]{2,1,0:T(1,128)S(1)}, u32[]{:S(2)}, u32[]{:S(2)}) collective-permute-start(f32[2,1,512]{2,1,0:T(1,128)S(1)} %get-tuple-element.68), channel_id=1, source_target_pairs={{0,2},{2,4},{4,6},{6,8},{8,10},{10,12},{12,14},{14,0},{1,3},{3,5},... | collective-permute-start | bytes 12296 | tf_op jit(solution)/shard_map/ppermute | solution.py:24
  107.9 8.4 %collective-permute-start.13 = (f32[2,192,1]{2,1,0:T(8,128)S(1)}, f32[2,192,1]{2,1,0:T(8,128)S(1)}, u32[]{:S(2)}, u32[]{:S(2)}) collective-permute-start(f32[2,192,1]{2,1,0:T(8,128)S(1)} %get-tuple-element.69), channel_id=1, source_target_pairs={{0,16},{16,32},{32,48},{48,64},{64,80},{80,96},{96,112},{112,128},... | collective-permute-start | bytes 4616 | tf_op jit(solution)/shard_map/ppermute | solution.py:24
  116.3 5.8 %collective-permute-start.12 = (f32[2,192,1]{2,1,0:T(8,128)S(1)}, f32[2,192,1]{2,1,0:T(8,128)S(1)}, u32[]{:S(2)}, u32[]{:S(2)}) collective-permute-start(f32[2,192,1]{2,1,0:T(8,128)S(1)} %get-tuple-element.70), channel_id=1, source_target_pairs={{16,0},{32,16},{48,32},{64,48},{80,64},{96,80},{112,96},{128,112},... | collective-permute-start | bytes 4616 | tf_op jit(solution)/shard_map/ppermute | solution.py:25
  171.1 22.6 %collective-permute-start.22 = (f32[1,192,512]{2,1,0:T(8,128)S(1)}, f32[1,192,512]{2,1,0:T(8,128)S(1)}, u32[]{:S(2)}, u32[]{:S(2)}) collective-permute-start(f32[1,192,512]{2,1,0:T(8,128)S(1)} %get-tuple-element.55), channel_id=1, source_target_pairs={{1,0},{3,2},{5,4},{7,6},{9,8},{11,10},{13,12},{15,14},{17,16},{19,... | collective-permute-start | bytes 1179656 | tf_op jit(solution)/shard_map/ppermute | solution.py:44
  172.6 21.2 %collective-permute-start.23 = (f32[1,192,512]{2,1,0:T(8,128)S(1)}, f32[1,192,512]{2,1,0:T(8,128)S(1)}, u32[]{:S(2)}, u32[]{:S(2)}) collective-permute-start(f32[1,192,512]{2,1,0:T(8,128)S(1)} %get-tuple-element.56), channel_id=1, source_target_pairs={{0,1},{2,3},{4,5},{6,7},{8,9},{10,11},{12,13},{14,15},{16,17},{18,... | collective-permute-start | bytes 1179656 | tf_op jit(solution)/shard_map/ppermute | solution.py:41
  176.6 17.2 %collective-permute-start.20 = (f32[2,1,512]{2,1,0:T(1,128)S(1)}, f32[2,1,512]{2,1,0:T(1,128)S(1)}, u32[]{:S(2)}, u32[]{:S(2)}) collective-permute-start(f32[2,1,512]{2,1,0:T(1,128)S(1)} %get-tuple-element.63), channel_id=1, source_target_pairs={{2,0},{4,2},{6,4},{8,6},{10,8},{12,10},{14,12},{0,14},{3,1},{5,3},... | collective-permute-start | bytes 12296 | tf_op jit(solution)/shard_map/ppermute | solution.py:25
  177.9 15.9 %collective-permute-start.21 = (f32[2,1,512]{2,1,0:T(1,128)S(1)}, f32[2,1,512]{2,1,0:T(1,128)S(1)}, u32[]{:S(2)}, u32[]{:S(2)}) collective-permute-start(f32[2,1,512]{2,1,0:T(1,128)S(1)} %get-tuple-element.64), channel_id=1, source_target_pairs={{0,2},{2,4},{4,6},{6,8},{8,10},{10,12},{12,14},{14,0},{1,3},{3,5},... | collective-permute-start | bytes 12296 | tf_op jit(solution)/shard_map/ppermute | solution.py:24
  178.3 9.7 %collective-permute-start.19 = (f32[2,192,1]{2,1,0:T(8,128)S(1)}, f32[2,192,1]{2,1,0:T(8,128)S(1)}, u32[]{:S(2)}, u32[]{:S(2)}) collective-permute-start(f32[2,192,1]{2,1,0:T(8,128)S(1)} %get-tuple-element.65), channel_id=1, source_target_pairs={{0,16},{16,32},{32,48},{48,64},{64,80},{80,96},{96,112},{112,128},... | collective-permute-start | bytes 4616 | tf_op jit(solution)/shard_map/ppermute | solution.py:24
  187.9 5.8 %collective-permute-start.18 = (f32[2,192,1]{2,1,0:T(8,128)S(1)}, f32[2,192,1]{2,1,0:T(8,128)S(1)}, u32[]{:S(2)}, u32[]{:S(2)}) collective-permute-start(f32[2,192,1]{2,1,0:T(8,128)S(1)} %get-tuple-element.66), channel_id=1, source_target_pairs={{16,0},{32,16},{48,32},{64,48},{80,64},{96,80},{112,96},{128,112},... | collective-permute-start | bytes 4616 | tf_op jit(solution)/shard_map/ppermute | solution.py:25
  (24 other events, 322.0 us)
where the time goes:
time: 247 us; the launch traced here: 243 us
  blocking collectives  118 us (48%)
  starting transfers between devices  67.4 us (27%)
  other arithmetic  23.9 us (10%)
  waiting for transfers between devices  17.5 us (7%)
  between operations  10.7 us (4%)
  local copies, waits for them, and re-layouts  5.05 us (2%)
    psum x15, blocking collectives, by_axis(): array = lax.psum(array, axis)  118 us
    ppermute x8, starting transfers between devices, padded(): lax.ppermute(last, axis, up)  24.7 us
    ppermute x8, starting transfers between devices, padded(): lax.ppermute(leading, axis, [(b, a) for a, b in up])  21.2 us
    ppermute x4, starting transfers between devices, padded_2(): lax.ppermute(lax.slice_in_dim(block, block.shape[dim] - width, None, axis...  16 us
    reduce_sum x3, other arithmetic, merged_sums(): jnp.sum(image_field * precond)  9.43 us
    ppermute x8, waiting for transfers between devices, padded(): lax.ppermute(leading, axis, [(b, a) for a, b in up])  8.73 us
    ppermute x8, waiting for transfers between devices, padded(): lax.ppermute(last, axis, up)  7.86 us
    sub x3, other arithmetic, shards(): residual = residual - step_size * image_dir  7.35 us
  transfers between devices with their start and end apart: 24, of which 8 were waited for; matrix products, arithmetic and copies ran while one was open for 2% of the time, Pallas kernels for 0%

commit v1 on v0

--- a/solution.py
+++ b/solution.py
@@ -4,7 +4,6 @@
 from jax.sharding import Mesh
 from jax.sharding import PartitionSpec as P
 
-ITERS = 3
 GX = ("gx_0", "gx_1")
 GY = ("gy_0", "gy_1")
 GX_GY_GZ = ("gx_0", "gx_1", "gy_0", "gy_1", "gz")
@@ -44,12 +43,6 @@
         high = lax.ppermute(lax.slice_in_dim(block, 0, width, axis=dim), axis, backward)
         block = jnp.concatenate([low, block, high], axis=dim)
     return block
-
-
-def by_axis(array, axes):
-    for axis in axes:
-        array = lax.psum(array, axis)
-    return array
 
 
 def lookup(classes, table):
@@ -99,13 +92,6 @@
     return padded_2(field, (("gz", 0),), 1)
 
 
-def merged_sums(residual, precond, image_field):
-    return (
-        by_axis(jnp.sum(residual * precond), GX_GY_GZ),
-        by_axis(jnp.sum(image_field * precond), GX_GY_GZ),
-    )
-
-
 def shards(load_current, sink_mask, pad_mask, plane_class, via_class, plane_table, via_table):
     n_layers, n_rows, n_cols = plane_class.shape
     g_plane = lookup(plane_class, plane_table)
@@ -136,45 +122,53 @@
     def precondition(residual):
         return solve_block(inverses, factors, up_edge, residual)
 
-    def operate(field):
+    def couple(field):
         inner = plane_extend(field)
         layer_ext = layer_extend(field)
-        above_field = layer_ext[2:]
-        below_field = layer_ext[:-2]
+        cross = jnp.concatenate(
+            [down_edge[:1] * layer_ext[:1]]
+            + [jnp.zeros_like(field[:1])] * (n_layers - 2)
+            + [up_edge[-1:] * layer_ext[-1:]],
+            0,
+        )
         return (
-            diagonal * field
-            - east_edge * inner[:, 1:-1, 2:]
-            - west_edge * inner[:, 1:-1, :-2]
-            - north_edge * inner[:, 2:, 1:-1]
-            - south_edge * inner[:, :-2, 1:-1]
-            - up_edge * above_field
-            - down_edge * below_field
+            east_edge * inner[:, 1:-1, 2:]
+            + west_edge * inner[:, 1:-1, :-2]
+            + north_edge * inner[:, 2:, 1:-1]
+            + south_edge * inner[:, :-2, 1:-1]
+            + cross
         )
 
+    def totals(*pairs):
+        return lax.psum(jnp.stack([jnp.sum(a * b) for a, b in pairs]), GX_GY_GZ)
+
     source = jnp.where(is_bottom, sink_mask.astype(jnp.float32) * load_current, jnp.float32(0.0))
-    right_side = jnp.concatenate(
+    s0 = jnp.concatenate(
         [source[None], jnp.zeros((n_layers - 1, n_rows, n_cols), jnp.float32)], 0
     )
-    voltage = jnp.zeros((n_layers, n_rows, n_cols), jnp.float32)
-    residual = right_side
-    precond = precondition(residual)
-    image_field = operate(precond)
-    weight_now, curvature = merged_sums(residual, precond, image_field)
-    step_size = weight_now / curvature
-    direction = precond
-    image_dir = image_field
-    for iteration in range(ITERS):
-        voltage = voltage + step_size * direction
-        residual = residual - step_size * image_dir
-        if iteration + 1 < ITERS:
-            precond = precondition(residual)
-            image_field = operate(precond)
-            weight_next, curvature = merged_sums(residual, precond, image_field)
-            momentum = weight_next / weight_now
-            step_size = weight_next / (curvature - momentum * weight_next / step_size)
-            direction = precond + momentum * direction
-            image_dir = image_field + momentum * image_dir
-            weight_now = weight_next
+    z0 = precondition(s0)
+    s1 = s0 - couple(z0)
+    mu, t00 = totals((z0, s0), (z0, s1))
+    step, shift = mu / t00, t00 / mu
+    z1 = z0 - step * precondition(s1)
+    r1 = s0 - step * s1
+    s2 = r1 - couple(z1)
+    z2 = precondition(s2) - shift * z1
+    s3 = (s2 - shift * r1) - couple(z2)
+    sums = totals((z0, s2), (z2, s1), (z1, s2), (z2, s2), (z2, s3), (z1, s0), (z2, s0))
+    t01, t02, t11, t12, t22, g1, g2 = sums / mu
+    t00 = shift
+    l1, l2 = t01 / t00, t02 / t00
+    d1, e1 = t11 - l1 * t01, t12 - l1 * t02
+    l3 = e1 / d1
+    d2 = t22 - l2 * t02 - l3 * e1
+    y1 = g1 - l1
+    y2 = g2 - l2 - l3 * y1
+    c2 = y2 / d2
+    c1 = y1 / d1 - l3 * c2
+    c0 = 1.0 / t00 - l1 * c1 - l2 * c2
+    voltage = c0 * z0 + c1 * z1 + c2 * z2
+    residual = s0 - c0 * s1 - c1 * s2 - c2 * s3
     return (voltage, residual)
 
 

time: 247 us -> 271 us (1.097); the launches traced: 243 us -> 270 us
  blocking collectives: 118 us -> 158 us
  starting transfers between devices: 67.4 us -> 49.4 us
  local copies, waits for them, and re-layouts: 5.05 us -> 11.5 us
  other arithmetic: 23.9 us -> 20.9 us
    psum x15 -> x2, blocking collectives: 118 us -> 158 us  [totals(): return lax.psum(jnp.stack([jnp.sum(a * b) for a, b in pairs]), GX_GY_GZ)]
    ppermute x8, starting transfers between devices: 24.7 us -> 8.08 us  [padded(): lax.ppermute(last, axis, up)]
    ppermute x4, waiting for transfers between devices: 0.92 us -> 9.14 us  [padded_2(): lax.ppermute(lax.slice_in_dim(block, 0, width, axis=dim), axis, backward)]
    ppermute x8, waiting for transfers between devices: 8.73 us -> 2.58 us  [padded(): lax.ppermute(leading, axis, [(b, a) for a, b in up])]
    another operation x0 -> x3, local copies, waits for them, and re-layouts: none -> 5.58 us  [the longest x1 4.35 us: totals(): return lax.psum(jnp.stack([jnp.sum(a * b) for a, b in pairs]), GX_GY_GZ)]
    ppermute x8, waiting for transfers between devices: 7.86 us -> 4.4 us  [padded(): lax.ppermute(last, axis, up)]
    reduce_sum x3 -> x2, other arithmetic: 9.43 us -> 6.14 us  [totals(): return lax.psum(jnp.stack([jnp.sum(a * b) for a, b in pairs]), GX_GY_GZ)]
    sub x3 -> x4, other arithmetic: 7.35 us -> 5.18 us  [the longest x1 3.72 us: shards(): residual = s0 - c0 * s1 - c1 * s2 - c2 * s3]
  transfers between devices with their start and end apart: 24 -> 24, of which waited for: 8 -> 10; matrix products, arithmetic and copies ran while one was open for 2% -> 1% of each run, Pallas kernels for 0% -> 0%
where the time goes in v1:
time: 271 us; the launch traced here: 270 us
  blocking collectives  158 us (58%)
  starting transfers between devices  49.4 us (18%)
  other arithmetic  20.9 us (8%)
  waiting for transfers between devices  18.5 us (7%)
  between operations  12 us (4%)
  local copies, waits for them, and re-layouts  11.5 us (4%)
    psum x2, blocking collectives, totals(): return lax.psum(jnp.stack([jnp.sum(a * b) for a, b in pairs]), GX_GY_GZ)  158 us
    ppermute x8, starting transfers between devices, padded(): lax.ppermute(leading, axis, [(b, a) for a, b in up])  22.3 us
    ppermute x4, starting transfers between devices, padded_2(): lax.ppermute(lax.slice_in_dim(block, block.shape[dim] - width, None, axis...  13.9 us
    ppermute x4, waiting for transfers between devices, padded_2(): lax.ppermute(lax.slice_in_dim(block, 0, width, axis=dim), axis, backward)  9.14 us
    ppermute x8, starting transfers between devices, padded(): lax.ppermute(last, axis, up)  8.08 us
    reduce_sum x2, other arithmetic, totals(): return lax.psum(jnp.stack([jnp.sum(a * b) for a, b in pairs]), GX_GY_GZ)  6.14 us
  transfers between devices with their start and end apart: 24, of which 10 were waited for; matrix products, arithmetic and copies ran while one was open for 1% of the time, Pallas kernels for 0%

profile of v1, /device:TPU:1, one launch (start us, length us, event | category | flops | bytes accessed | tf_op | source)
XLA Modules:
  0.0 270.3 jit_solution(9392913492535320688)
XLA Ops:
  1.9 1.9 select_add_fusion.1
  3.9 3.0 %collective-permute-start = (f32[2,192,1]{2,1,0:T(8,128)S(1)}, f32[2,192,1]{2,1,0:T(8,128)S(1)}, u32[]{:S(2)}, u32[]{:S(2)}) collective-permute-start(f32[2,192,1]{2,1,0:T(8,128)S(1)} %get-tuple-element.59), channel_id=1, source_target_pairs={{0,16},{16,32},{32,48},{48,64},{64,80},{80,96},{96,112},{112,128},... | collective-permute-start | bytes 4616 | tf_op jit(solution)/shard_map/ppermute | solution.py:23
  11.1 3.9 %collective-permute-start.4 = (f32[1,192,512]{2,1,0:T(8,128)}, f32[1,192,512]{2,1,0:T(8,128)}, u32[]{:S(2)}, u32[]{:S(2)}) collective-permute-start(f32[1,192,512]{2,1,0:T(8,128)} %get-tuple-element.61), channel_id=1, source_target_pairs={{0,1},{2,3},{4,5},{6,7},{8,9},{10,11},{12,13},{14,15},{16,17},{18,... | collective-permute-start | bytes 1179656 | tf_op jit(solution)/shard_map/ppermute | solution.py:40
  16.3 4.5 %collective-permute-start.3 = (f32[2,1,512]{2,1,0:T(1,128)S(1)}, f32[2,1,512]{2,1,0:T(1,128)S(1)}, u32[]{:S(2)}, u32[]{:S(2)}) collective-permute-start(f32[2,1,512]{2,1,0:T(1,128)S(1)} %get-tuple-element.58), channel_id=1, source_target_pairs={{2,0},{4,2},{6,4},{8,6},{10,8},{12,10},{14,12},{0,14},{3,1},{5,3},... | collective-permute-start | bytes 12296 | tf_op jit(solution)/shard_map/ppermute | solution.py:24
  21.8 2.2 collective-permute-done.5
  28.8 4.0 %collective-permute-start.10 = (f32[1,192,512]{2,1,0:T(8,128)S(1)}, f32[1,192,512]{2,1,0:T(8,128)S(1)}, u32[]{:S(2)}, u32[]{:S(2)}) collective-permute-start(f32[1,192,512]{2,1,0:T(8,128)S(1)} %get-tuple-element.33), channel_id=1, source_target_pairs={{0,1},{2,3},{4,5},{6,7},{8,9},{10,11},{12,13},{14,15},{16,17},{18,... | collective-permute-start | bytes 1179656 | tf_op jit(solution)/shard_map/ppermute | solution.py:40
  32.8 4.3 %collective-permute-start.8 = (f32[2,1,512]{2,1,0:T(1,128)S(1)}, f32[2,1,512]{2,1,0:T(1,128)S(1)}, u32[]{:S(2)}, u32[]{:S(2)}) collective-permute-start(f32[2,1,512]{2,1,0:T(1,128)S(1)} %get-tuple-element.53), channel_id=1, source_target_pairs={{2,0},{4,2},{6,4},{8,6},{10,8},{12,10},{14,12},{0,14},{3,1},{5,3},... | collective-permute-start | bytes 12296 | tf_op jit(solution)/shard_map/ppermute | solution.py:24
  37.2 6.4 %collective-permute-start.6 = (f32[2,192,1]{2,1,0:T(8,128)S(1)}, f32[2,192,1]{2,1,0:T(8,128)S(1)}, u32[]{:S(2)}, u32[]{:S(2)}) collective-permute-start(f32[2,192,1]{2,1,0:T(8,128)S(1)} %get-tuple-element.56), channel_id=1, source_target_pairs={{16,0},{32,16},{48,32},{64,48},{80,64},{96,80},{112,96},{128,112},... | collective-permute-start | bytes 4616 | tf_op jit(solution)/shard_map/ppermute | solution.py:24
  43.6 2.0 collective-permute-start.7
  45.7 2.2 collective-permute-done.6
  48.2 2.9 %fusion.2 = (f32[]{:T(128)}, f32[]{:T(128)}, f32[2,192,512]{2,1,0:T(8,128)}) fusion(f32[1,192,512]{2,1,0:T(8,128)S(1)} %bitcast.68, f32[1,192,512]{2,1,0:T(8,128)S(1)} %get-tuple-element.33, f32[1,192,512]{2,1,0:T(8,128)S(1)} %subtract_bitcast_fusion, f32[1,192,512]{2,1,0:T(8,128)S(1)} %get-tuple-element.40, f32[1,192,512]{2,1,0:T(8,128)S(1)} %get-tuple-element.39, ...), kind=kLoop, calls=%fused_computation.32 | loop fusion | flops 6488062 | bytes 5909512 | tf_op jit(solution)/shard_map/reduce_sum | solution.py:143
  52.4 79.5 %psum.14 = f32[2]{0:T(128)S(1)} all-reduce(f32[2]{0:T(128)S(1)} %pad_maximum_fusion.31), channel_id=1, replica_groups=mesh['gx_0'=8,'gx_1'=2,'gy_0'=2,'gy_1'=4,'gz'=2] {'gx_0','gx_1','gy_0','..., use_global_device_ids=true, to_apply=%region_2.3 | all-reduce | flops 2 | bytes 16 | tf_op jit(solution)/shard_map/psum | solution.py:143
  141.8 2.5 collective-permute-start.14
  144.3 2.0 collective-permute-done.16
  146.4 3.8 %collective-permute-done.17 = f32[1,192,512]{2,1,0:T(8,128)S(1)} collective-permute-done((f32[1,192,512]{2,1,0:T(8,128)S(1)}, f32[1,192,512]{2,1,0:T(8,128)S(1)}, u32[]{:S(2)}, u32[]{:S(2)}) %collective-permute-start.17) | collective-permute-done | bytes 393248 | tf_op jit(solution)/shard_map/ppermute | solution.py:43
  150.4 2.0 collective-permute-done.15
  154.7 4.1 %collective-permute-start.22 = (f32[1,192,512]{2,1,0:T(8,128)S(1)}, f32[1,192,512]{2,1,0:T(8,128)S(1)}, u32[]{:S(2)}, u32[]{:S(2)}) collective-permute-start(f32[1,192,512]{2,1,0:T(8,128)S(1)} %get-tuple-element.45), channel_id=1, source_target_pairs={{0,1},{2,3},{4,5},{6,7},{8,9},{10,11},{12,13},{14,15},{16,17},{18,... | collective-permute-start | bytes 1179656 | tf_op jit(solution)/shard_map/ppermute | solution.py:40
  160.3 3.0 %collective-permute-start.18 = (f32[2,192,1]{2,1,0:T(8,128)S(1)}, f32[2,192,1]{2,1,0:T(8,128)S(1)}, u32[]{:S(2)}, u32[]{:S(2)}) collective-permute-start(f32[2,192,1]{2,1,0:T(8,128)S(1)} %get-tuple-element.44), channel_id=1, source_target_pairs={{16,0},{32,16},{48,32},{64,48},{80,64},{96,80},{112,96},{128,112},... | collective-permute-start | bytes 4616 | tf_op jit(solution)/shard_map/ppermute | solution.py:24
  165.3 3.1 %collective-permute-done.23 = f32[1,192,512]{2,1,0:T(8,128)S(1)} collective-permute-done((f32[1,192,512]{2,1,0:T(8,128)S(1)}, f32[1,192,512]{2,1,0:T(8,128)S(1)}, u32[]{:S(2)}, u32[]{:S(2)}) %collective-permute-start.23) | collective-permute-done | bytes 393248 | tf_op jit(solution)/shard_map/ppermute | solution.py:43
  168.6 2.0 collective-permute-done.21
  170.7 3.3 %fusion.4 = (f32[]{:T(128)}, f32[]{:T(128)}, f32[]{:T(128)}, f32[]{:T(128)}, f32[]{:T(128)}, /*index=5*/f32[]{:T(128)}, f32[]{:T(128)}, f32[2,192,512]{2,1,0:T(8,128)}) fusion(f32[2,192,512]{2,1,0:T(8,128)S(1)} %maximum_subtract_fusion, f32[1,192,512]{2,1,0:T(8,128)S(1)} %bitcast.71, f32[2,192,512]{2,1,0:T(8,128)S(1)} %fusion.22, ...), kind=kLoop, calls=%fused_computation.34 | loop fusion | flops 9043961 | bytes 9055268 | tf_op jit(solution)/shard_map/reduce_sum | solution.py:143
  173.9 4.3 %stack.67 = f32[7]{0:T(128)S(1)} concatenate(f32[1]{0:T(128)} %bitcast.11, f32[1]{0:T(128)} %bitcast.12, f32[1]{0:T(128)} %bitcast.13, f32[1]{0:T(128)} %bitcast.14, f32[1]{0:T(128)} %bitcast.15, f32[1]{0:T(128)} %bitcast.16, f32[1]{0:T(128)} %bitcast.17), dimensions={0} | concatenate | bytes 56 | tf_op jit(solution)/shard_map/stack | solution.py:143
  178.3 78.4 %psum.15 = f32[7]{0:T(128)S(1)} all-reduce(f32[7]{0:T(128)S(1)} %stack.67), channel_id=1, replica_groups=mesh['gx_0'=8,'gx_1'=2,'gy_0'=2,'gy_1'=4,'gz'=2] {'gx_0','gx_1','gy_0','..., use_global_device_ids=true, to_apply=%region_10.11 | all-reduce | flops 7 | bytes 56 | tf_op jit(solution)/shard_map/psum | solution.py:143
  266.5 3.7 %fusion.6 = (f32[2,192,512]{2,1,0:T(8,128)}, f32[2,192,512]{2,1,0:T(8,128)}) fusion(f32[1,192,512]{2,1,0:T(8,128)} %bitcast.69, f32[2,192,512]{2,1,0:T(8,128)} %get-tuple-element.27, f32[2,192,512]{2,1,0:T(8,128)} %copy-done.9, f32[2,192,512]{2,1,0:T(8,128)S(1)} %copy-done.4, f32[]{:T(128)S(6)} %div.71, f32[]{:T(128)S(6)} %sub.88, f32[]{:T(128)S(6)} %sub.90, ...), kind=kLoop, calls=%fused_computation.36 | loop fusion | flops 3538944 | bytes 6684692 | tf_op jit(solution)/shard_map/sub | solution.py:171
  (106 shorter events, 29.2 us)
Async XLA Ops:
  3.9 12.4 %collective-permute-start = (f32[2,192,1]{2,1,0:T(8,128)S(1)}, f32[2,192,1]{2,1,0:T(8,128)S(1)}, u32[]{:S(2)}, u32[]{:S(2)}) collective-permute-start(f32[2,192,1]{2,1,0:T(8,128)S(1)} %get-tuple-element.59), channel_id=1, source_target_pairs={{0,16},{16,32},{32,48},{48,64},{64,80},{80,96},{96,112},{112,128},... | collective-permute-start | bytes 4616 | tf_op jit(solution)/shard_map/ppermute | solution.py:23
  6.9 13.8 %collective-permute-start.1 = (f32[2,192,1]{2,1,0:T(8,128)S(1)}, f32[2,192,1]{2,1,0:T(8,128)S(1)}, u32[]{:S(2)}, u32[]{:S(2)}) collective-permute-start(f32[2,192,1]{2,1,0:T(8,128)S(1)} %get-tuple-element.60), channel_id=1, source_target_pairs={{16,0},{32,16},{48,32},{64,48},{80,64},{96,80},{112,96},{128,112},... | collective-permute-start | bytes 4616 | tf_op jit(solution)/shard_map/ppermute | solution.py:24
  7.2 14.0 %collective-permute-start.2 = (f32[2,1,512]{2,1,0:T(1,128)S(1)}, f32[2,1,512]{2,1,0:T(1,128)S(1)}, u32[]{:S(2)}, u32[]{:S(2)}) collective-permute-start(f32[2,1,512]{2,1,0:T(1,128)S(1)} %get-tuple-element.57), channel_id=1, source_target_pairs={{0,2},{2,4},{4,6},{6,8},{8,10},{10,12},{12,14},{14,0},{1,3},{3,5},... | collective-permute-start | bytes 12296 | tf_op jit(solution)/shard_map/ppermute | solution.py:23
  11.1 10.7 %collective-permute-start.4 = (f32[1,192,512]{2,1,0:T(8,128)}, f32[1,192,512]{2,1,0:T(8,128)}, u32[]{:S(2)}, u32[]{:S(2)}) collective-permute-start(f32[1,192,512]{2,1,0:T(8,128)} %get-tuple-element.61), channel_id=1, source_target_pairs={{0,1},{2,3},{4,5},{6,7},{8,9},{10,11},{12,13},{14,15},{16,17},{18,... | collective-permute-start | bytes 1179656 | tf_op jit(solution)/shard_map/ppermute | solution.py:40
  14.9 9.0 %collective-permute-start.5 = (f32[1,192,512]{2,1,0:T(8,128)}, f32[1,192,512]{2,1,0:T(8,128)}, u32[]{:S(2)}, u32[]{:S(2)}) collective-permute-start(f32[1,192,512]{2,1,0:T(8,128)} %get-tuple-element.62), channel_id=1, source_target_pairs={{1,0},{3,2},{5,4},{7,6},{9,8},{11,10},{13,12},{15,14},{17,16},{19,... | collective-permute-start | bytes 1179656 | tf_op jit(solution)/shard_map/ppermute | solution.py:43
  16.3 5.2 %collective-permute-start.3 = (f32[2,1,512]{2,1,0:T(1,128)S(1)}, f32[2,1,512]{2,1,0:T(1,128)S(1)}, u32[]{:S(2)}, u32[]{:S(2)}) collective-permute-start(f32[2,1,512]{2,1,0:T(1,128)S(1)} %get-tuple-element.58), channel_id=1, source_target_pairs={{2,0},{4,2},{6,4},{8,6},{10,8},{12,10},{14,12},{0,14},{3,1},{5,3},... | collective-permute-start | bytes 12296 | tf_op jit(solution)/shard_map/ppermute | solution.py:24
  27.5 16.1 %collective-permute-start.11 = (f32[1,192,512]{2,1,0:T(8,128)S(1)}, f32[1,192,512]{2,1,0:T(8,128)S(1)}, u32[]{:S(2)}, u32[]{:S(2)}) collective-permute-start(f32[1,192,512]{2,1,0:T(8,128)S(1)} %subtract_bitcast_fusion), channel_id=1, source_target_pairs={{1,0},{3,2},{5,4},{7,6},{9,8},{11,10},{13,12},{15,14},{17,16},{19,... | collective-permute-start | bytes 1179656 | tf_op jit(solution)/shard_map/ppermute | solution.py:43
  28.8 16.8 %collective-permute-start.10 = (f32[1,192,512]{2,1,0:T(8,128)S(1)}, f32[1,192,512]{2,1,0:T(8,128)S(1)}, u32[]{:S(2)}, u32[]{:S(2)}) collective-permute-start(f32[1,192,512]{2,1,0:T(8,128)S(1)} %get-tuple-element.33), channel_id=1, source_target_pairs={{0,1},{2,3},{4,5},{6,7},{8,9},{10,11},{12,13},{14,15},{16,17},{18,... | collective-permute-start | bytes 1179656 | tf_op jit(solution)/shard_map/ppermute | solution.py:40
  32.8 15.3 %collective-permute-start.8 = (f32[2,1,512]{2,1,0:T(1,128)S(1)}, f32[2,1,512]{2,1,0:T(1,128)S(1)}, u32[]{:S(2)}, u32[]{:S(2)}) collective-permute-start(f32[2,1,512]{2,1,0:T(1,128)S(1)} %get-tuple-element.53), channel_id=1, source_target_pairs={{2,0},{4,2},{6,4},{8,6},{10,8},{12,10},{14,12},{0,14},{3,1},{5,3},... | collective-permute-start | bytes 12296 | tf_op jit(solution)/shard_map/ppermute | solution.py:24
  37.1 11.1 %collective-permute-start.9 = (f32[2,1,512]{2,1,0:T(1,128)S(1)}, f32[2,1,512]{2,1,0:T(1,128)S(1)}, u32[]{:S(2)}, u32[]{:S(2)}) collective-permute-start(f32[2,1,512]{2,1,0:T(1,128)S(1)} %get-tuple-element.54), channel_id=1, source_target_pairs={{0,2},{2,4},{4,6},{6,8},{8,10},{10,12},{12,14},{14,0},{1,3},{3,5},... | collective-permute-start | bytes 12296 | tf_op jit(solution)/shard_map/ppermute | solution.py:23
  37.2 10.6 %collective-permute-start.6 = (f32[2,192,1]{2,1,0:T(8,128)S(1)}, f32[2,192,1]{2,1,0:T(8,128)S(1)}, u32[]{:S(2)}, u32[]{:S(2)}) collective-permute-start(f32[2,192,1]{2,1,0:T(8,128)S(1)} %get-tuple-element.56), channel_id=1, source_target_pairs={{16,0},{32,16},{48,32},{64,48},{80,64},{96,80},{112,96},{128,112},... | collective-permute-start | bytes 4616 | tf_op jit(solution)/shard_map/ppermute | solution.py:24
  43.6 4.6 %collective-permute-start.7 = (f32[2,192,1]{2,1,0:T(8,128)S(1)}, f32[2,192,1]{2,1,0:T(8,128)S(1)}, u32[]{:S(2)}, u32[]{:S(2)}) collective-permute-start(f32[2,192,1]{2,1,0:T(8,128)S(1)} %get-tuple-element.55), channel_id=1, source_target_pairs={{0,16},{16,32},{32,48},{48,64},{64,80},{80,96},{96,112},{112,128},... | collective-permute-start | bytes 4616 | tf_op jit(solution)/shard_map/ppermute | solution.py:23
  136.8 9.6 %collective-permute-start.16 = (f32[1,192,512]{2,1,0:T(8,128)S(1)}, f32[1,192,512]{2,1,0:T(8,128)S(1)}, u32[]{:S(2)}, u32[]{:S(2)}) collective-permute-start(f32[1,192,512]{2,1,0:T(8,128)S(1)} %get-tuple-element.47), channel_id=1, source_target_pairs={{0,1},{2,3},{4,5},{6,7},{8,9},{10,11},{12,13},{14,15},{16,17},{18,... | collective-permute-start | bytes 1179656 | tf_op jit(solution)/shard_map/ppermute | solution.py:40
  138.6 11.6 %collective-permute-start.17 = (f32[1,192,512]{2,1,0:T(8,128)S(1)}, f32[1,192,512]{2,1,0:T(8,128)S(1)}, u32[]{:S(2)}, u32[]{:S(2)}) collective-permute-start(f32[1,192,512]{2,1,0:T(8,128)S(1)} %get-tuple-element.48), channel_id=1, source_target_pairs={{1,0},{3,2},{5,4},{7,6},{9,8},{11,10},{13,12},{15,14},{17,16},{19,... | collective-permute-start | bytes 1179656 | tf_op jit(solution)/shard_map/ppermute | solution.py:43
  140.0 10.3 %collective-permute-start.12 = (f32[2,192,1]{2,1,0:T(8,128)S(1)}, f32[2,192,1]{2,1,0:T(8,128)S(1)}, u32[]{:S(2)}, u32[]{:S(2)}) collective-permute-start(f32[2,192,1]{2,1,0:T(8,128)S(1)} %get-tuple-element.52), channel_id=1, source_target_pairs={{16,0},{32,16},{48,32},{64,48},{80,64},{96,80},{112,96},{128,112},... | collective-permute-start | bytes 4616 | tf_op jit(solution)/shard_map/ppermute | solution.py:24
  141.0 9.4 %collective-permute-start.13 = (f32[2,192,1]{2,1,0:T(8,128)S(1)}, f32[2,192,1]{2,1,0:T(8,128)S(1)}, u32[]{:S(2)}, u32[]{:S(2)}) collective-permute-start(f32[2,192,1]{2,1,0:T(8,128)S(1)} %get-tuple-element.51), channel_id=1, source_target_pairs={{0,16},{16,32},{32,48},{48,64},{64,80},{80,96},{96,112},{112,128},... | collective-permute-start | bytes 4616 | tf_op jit(solution)/shard_map/ppermute | solution.py:23
  141.8 8.6 %collective-permute-start.14 = (f32[2,1,512]{2,1,0:T(1,128)S(1)}, f32[2,1,512]{2,1,0:T(1,128)S(1)}, u32[]{:S(2)}, u32[]{:S(2)}) collective-permute-start(f32[2,1,512]{2,1,0:T(1,128)S(1)} %get-tuple-element.49), channel_id=1, source_target_pairs={{2,0},{4,2},{6,4},{8,6},{10,8},{12,10},{14,12},{0,14},{3,1},{5,3},... | collective-permute-start | bytes 12296 | tf_op jit(solution)/shard_map/ppermute | solution.py:24
  146.4 6.1 %collective-permute-start.15 = (f32[2,1,512]{2,1,0:T(1,128)S(1)}, f32[2,1,512]{2,1,0:T(1,128)S(1)}, u32[]{:S(2)}, u32[]{:S(2)}) collective-permute-start(f32[2,1,512]{2,1,0:T(1,128)S(1)} %get-tuple-element.50), channel_id=1, source_target_pairs={{0,2},{2,4},{4,6},{6,8},{8,10},{10,12},{12,14},{14,0},{1,3},{3,5},... | collective-permute-start | bytes 12296 | tf_op jit(solution)/shard_map/ppermute | solution.py:23
  154.7 9.8 %collective-permute-start.22 = (f32[1,192,512]{2,1,0:T(8,128)S(1)}, f32[1,192,512]{2,1,0:T(8,128)S(1)}, u32[]{:S(2)}, u32[]{:S(2)}) collective-permute-start(f32[1,192,512]{2,1,0:T(8,128)S(1)} %get-tuple-element.45), channel_id=1, source_target_pairs={{0,1},{2,3},{4,5},{6,7},{8,9},{10,11},{12,13},{14,15},{16,17},{18,... | collective-permute-start | bytes 1179656 | tf_op jit(solution)/shard_map/ppermute | solution.py:40
  158.9 9.6 %collective-permute-start.23 = (f32[1,192,512]{2,1,0:T(8,128)S(1)}, f32[1,192,512]{2,1,0:T(8,128)S(1)}, u32[]{:S(2)}, u32[]{:S(2)}) collective-permute-start(f32[1,192,512]{2,1,0:T(8,128)S(1)} %get-tuple-element.46), channel_id=1, source_target_pairs={{1,0},{3,2},{5,4},{7,6},{9,8},{11,10},{13,12},{15,14},{17,16},{19,... | collective-permute-start | bytes 1179656 | tf_op jit(solution)/shard_map/ppermute | solution.py:43
  160.3 8.3 %collective-permute-start.18 = (f32[2,192,1]{2,1,0:T(8,128)S(1)}, f32[2,192,1]{2,1,0:T(8,128)S(1)}, u32[]{:S(2)}, u32[]{:S(2)}) collective-permute-start(f32[2,192,1]{2,1,0:T(8,128)S(1)} %get-tuple-element.44), channel_id=1, source_target_pairs={{16,0},{32,16},{48,32},{64,48},{80,64},{96,80},{112,96},{128,112},... | collective-permute-start | bytes 4616 | tf_op jit(solution)/shard_map/ppermute | solution.py:24
  163.3 5.3 %collective-permute-start.19 = (f32[2,192,1]{2,1,0:T(8,128)S(1)}, f32[2,192,1]{2,1,0:T(8,128)S(1)}, u32[]{:S(2)}, u32[]{:S(2)}) collective-permute-start(f32[2,192,1]{2,1,0:T(8,128)S(1)} %get-tuple-element.43), channel_id=1, source_target_pairs={{0,16},{16,32},{32,48},{48,64},{64,80},{80,96},{96,112},{112,128},... | collective-permute-start | bytes 4616 | tf_op jit(solution)/shard_map/ppermute | solution.py:23
  163.8 4.8 %collective-permute-start.20 = (f32[2,1,512]{2,1,0:T(1,128)S(1)}, f32[2,1,512]{2,1,0:T(1,128)S(1)}, u32[]{:S(2)}, u32[]{:S(2)}) collective-permute-start(f32[2,1,512]{2,1,0:T(1,128)S(1)} %get-tuple-element.41), channel_id=1, source_target_pairs={{2,0},{4,2},{6,4},{8,6},{10,8},{12,10},{14,12},{0,14},{3,1},{5,3},... | collective-permute-start | bytes 12296 | tf_op jit(solution)/shard_map/ppermute | solution.py:24
  164.6 6.1 %collective-permute-start.21 = (f32[2,1,512]{2,1,0:T(1,128)S(1)}, f32[2,1,512]{2,1,0:T(1,128)S(1)}, u32[]{:S(2)}, u32[]{:S(2)}) collective-permute-start(f32[2,1,512]{2,1,0:T(1,128)S(1)} %get-tuple-element.42), channel_id=1, source_target_pairs={{0,2},{2,4},{4,6},{6,8},{8,10},{10,12},{12,14},{14,0},{1,3},{3,5},... | collective-permute-start | bytes 12296 | tf_op jit(solution)/shard_map/ppermute | solution.py:23
  (21 other events, 361.9 us)

commit v2 on v1

v2 whole, which is shorter than its diff:
```python
import functools

import jax
import jax.numpy as jnp
from jax import lax
from jax.experimental import pallas as pl
from jax.experimental.pallas import tpu as pltpu
from jax.sharding import PartitionSpec as P

PAD_CONDUCTANCE = 20.0
MESH = pl.DeviceIdType.MESH
HALO = 8
LANES = 128
F32 = jnp.float32


def harmonic(first, second):
    return 2.0 * first * second / (first + second)


def pick(classes, table):
    low = (classes & 1) == 1
    mid = (classes & 2) == 2
    high = (classes & 4) == 4
    pairs = [jnp.where(low, table[2 * k + 1], table[2 * k]) for k in range(4)]
    return jnp.where(
        high, jnp.where(mid, pairs[3], pairs[2]), jnp.where(mid, pairs[1], pairs[0])
    )


def kernel(
    sizes,
    load_ref, sink_ref, pad_ref, plane_ref, via_ref, plane_tab, via_tab,
    volt_ref, resid_ref,
    class_n, class_s, class_e, class_w, via_other, tab_other,
    g_buf, g_e, g_w,
    east, west, north, south, cross, inv0, inv1, mix, src,
    z0, z0_e, z0_w, z0_o, y1, y1_e, y1_w, y1_o, z1, z1_e, z1_w, z1_o, z2, z2_e, z2_w, z2_o,
    s1, s2, q2, s3,
    part, got_x, got_y, got_z, send_sem, recv_sem,
):
    nx, ny, rows, cols = sizes
    strips = rows // 8
    ix, iy, iz = lax.axis_index("gx"), lax.axis_index("gy"), lax.axis_index("gz")
    gx_up, gx_dn = lax.rem(ix + 1, nx), lax.rem(ix + nx - 1, nx)
    gy_up, gy_dn = lax.rem(iy + 1, ny), lax.rem(iy + ny - 1, ny)
    other = 1 - iz
    used = [0]

    def copy(source, target, where_to):
        k = used[0]
        used[0] += 1
        return pltpu.make_async_remote_copy(
            src_ref=source, dst_ref=target, send_sem=send_sem.at[k], recv_sem=recv_sem.at[k],
            device_id=where_to, device_id_type=MESH,
        )

    barrier = pltpu.get_barrier_semaphore()
    peers = [{"gx": lax.rem(ix + k, nx)} for k in range(1, nx)]
    peers += [{"gy": lax.rem(iy + k, ny)} for k in range(1, ny)]
    peers += [{"gz": other}]
    for peer in peers:
        pl.semaphore_signal(barrier, inc=1, device_id=peer, device_id_type=MESH)
    pl.semaphore_wait(barrier, len(peers))

    first = [
        copy(via_ref.at[other], via_other, {"gz": other}),
        copy(via_tab, tab_other, {"gz": other}),
        copy(plane_ref.at[:, pl.ds(rows - 8, 8), :], class_s, {"gy": gy_up}),
        copy(plane_ref.at[:, pl.ds(0, 8), :], class_n, {"gy": gy_dn}),
        copy(plane_ref.at[:, :, pl.ds(cols - LANES, LANES)], class_w, {"gx": gx_up}),
        copy(plane_ref.at[:, :, pl.ds(0, LANES)], class_e, {"gx": gx_dn}),
    ]
    for c in first:
        c.start()

    def own_table(tab, slot):
        line = jnp.where(iz == 0, tab[slot : slot + 1, :], tab[1 - slot : 2 - slot, :])
        return [line[:, k : k + 1] for k in range(8)]

    plane_of = [own_table(plane_tab, slot) for slot in (0, 1)]
    via_of = [own_table(via_tab, slot) for slot in (0, 1)]
    layer = (iz, other)

    def at(i):
        return pl.ds(pl.multiple_of(i * 8, 8), 8)

    def inner(i):
        return pl.ds(pl.multiple_of(i * 8 + HALO, 8), 8)

    def lookup_own(i, _):
        for slot in (0, 1):
            g_buf[slot, inner(i), :] = pick(plane_ref[layer[slot], at(i), :], plane_of[slot])
        return 0

    lax.fori_loop(0, strips, lookup_own, 0)
    for c in first:
        c.wait()
    for slot in (0, 1):
        g_buf[slot, 0:HALO, :] = pick(class_s[layer[slot]], plane_of[slot])
        g_buf[slot, HALO + rows : 2 * HALO + rows, :] = pick(class_n[layer[slot]], plane_of[slot])

    other_line = jnp.where(iz == 0, tab_other[0:1, :], tab_other[1:2, :])
    other_of = [other_line[:, k : k + 1] for k in range(8)]

    def lookup_sides(i, _):
        for slot in (0, 1):
            g_e[slot, at(i), :] = pick(class_e[layer[slot], at(i), :], plane_of[slot])
            g_w[slot, at(i), :] = pick(class_w[layer[slot], at(i), :], plane_of[slot])
        return 0

    lax.fori_loop(0, strips, lookup_sides, 0)

    def around(buf, buf_e, buf_w, slot, i):
        here = buf[slot, inner(i), :]
        below = buf[slot, pl.ds(pl.multiple_of(i * 8, 8), 8), :]
        above = buf[slot, pl.ds(pl.multiple_of(i * 8 + 2 * HALO, 8), 8), :]
        up = jnp.concatenate([here[1:], above[:1]], 0)
        down = jnp.concatenate([below[7:], here[:7]], 0)
        right = pltpu.roll(
            jnp.concatenate([here, buf_e[slot, at(i), :]], 1), cols + LANES - 1, 1
        )[:, :cols]
        left = pltpu.roll(jnp.concatenate([buf_w[slot, at(i), :], here], 1), 1, 1)[:, LANES:]
        return here, right, left, up, down

    is_source = jnp.where(iz == 0, F32(1.0), F32(0.0))
    pad_scale = jnp.where(iz == 0, F32(0.0), F32(PAD_CONDUCTANCE))

    def solve(i, b0, b1):
        i0, i1, m = inv0[at(i), :], inv1[at(i), :], mix[at(i), :]
        x1 = (b1 + m * b0) * i1
        return b0 * i0 + m * x1, x1

    def build(i, _):
        sums = []
        for slot in (0, 1):
            here, right, left, up, down = around(g_buf, g_e, g_w, slot, i)
            edges = [harmonic(here, near) for near in (right, left, up, down)]
            for ref, value in zip((east, west, north, south), edges):
                ref[slot, at(i), :] = value
            sums.append(edges[0] + edges[1] + edges[2] + edges[3])
        via0 = pick(via_ref[layer[0], at(i), :], via_of[0])
        via1 = pick(via_ref[layer[1], at(i), :], via_of[1])
        link = harmonic(via0, via1)
        far = harmonic(via1, pick(via_other[at(i), :], other_of))
        cross[at(i), :] = far
        d0 = sums[0] + link + pad_scale * pad_ref[at(i), :].astype(F32)
        d1 = sums[1] + link + far
        i0 = 1.0 / d0
        m = link * i0
        i1 = 1.0 / (d1 - link * m)
        inv0[at(i), :] = i0
        inv1[at(i), :] = i1
        mix[at(i), :] = m
        b0 = is_source * (sink_ref[at(i), :].astype(F32) * load_ref[at(i), :])
        src[at(i), :] = b0
        x1 = m * b0 * i1
        z0[0, inner(i), :] = b0 * i0 + m * x1
        z0[1, inner(i), :] = x1
        return 0

    lax.fori_loop(0, strips, build, 0)

    def exchange(buf, buf_e, buf_w, buf_o):
        moves = [
            copy(buf.at[1, pl.ds(HALO, rows), :], buf_o, {"gz": other}),
            copy(buf.at[:, pl.ds(rows, 8), :], buf.at[:, pl.ds(0, 8), :], {"gy": gy_up}),
            copy(buf.at[:, pl.ds(HALO, 8), :], buf.at[:, pl.ds(HALO + rows, 8), :], {"gy": gy_dn}),
            copy(buf.at[:, pl.ds(HALO, rows), pl.ds(cols - LANES, LANES)], buf_w, {"gx": gx_up}),
            copy(buf.at[:, pl.ds(HALO, rows), pl.ds(0, LANES)], buf_e, {"gx": gx_dn}),
        ]
        for c in moves:
            c.start()
        return moves

    def couple(buf, buf_e, buf_w, buf_o, i):
        out = []
        for slot in (0, 1):
            here, right, left, up, down = around(buf, buf_e, buf_w, slot, i)
            u = (
                east[slot, at(i), :] * right + west[slot, at(i), :] * left
                + north[slot, at(i), :] * up + south[slot, at(i), :] * down
            )
            if slot == 1:
                u = u + cross[at(i), :] * buf_o[at(i), :]
            out.append((here, u))
        return out

    lane = lax.broadcasted_iota(jnp.int32, (1, LANES), 1)

    def all_sum(which, sums):
        line = jnp.zeros((1, LANES), F32)
        for k, value in enumerate(sums):
            line = jnp.where(lane == k, jnp.sum(value), line)
        for stage, (axis, size, me, got) in enumerate(
            (("gx", nx, ix, got_x), ("gy", ny, iy, got_y), ("gz", 2, iz, got_z))
        ):
            part[which, stage] = line
            got[which, me] = line
            moves = [
                copy(part.at[which, stage], got.at[which, me], {axis: lax.rem(me + k, size)})
                for k in range(1, size)
            ]
            for c in moves:
                c.start()
            for c in moves:
                c.wait()
            line = got[which, 0]
            for k in range(1, size):
                line = line + got[which, k]
        return [
            jnp.sum(jnp.where(lane == k, line, 0.0), axis=1, keepdims=True)
            for k in range(len(sums))
        ]

    zero = jnp.zeros((8, cols), F32)

    for c in exchange(z0, z0_e, z0_w, z0_o):
        c.wait()

    def pass1(i, carry):
        (h0, u0), (h1, u1) = couple(z0, z0_e, z0_w, z0_o, i)
        b0 = src[at(i), :]
        a0, a1 = b0 - u0, -u1
        s1[0, at(i), :] = a0
        s1[1, at(i), :] = a1
        x0, x1 = solve(i, a0, a1)
        y1[0, inner(i), :] = x0
        y1[1, inner(i), :] = x1
        return carry[0] + h0 * b0, carry[1] + (h0 * a0 + h1 * a1)

    sums = lax.fori_loop(0, strips, pass1, (zero, zero))
    moves = exchange(y1, y1_e, y1_w, y1_o)
    mu, t00 = all_sum(0, sums)
    for c in moves:
        c.wait()
    step, shift = mu / t00, t00 / mu

    def blend(i, _):
        for slot in (0, 1):
            for a, b, c in ((z0_e, y1_e, z1_e), (z0_w, y1_w, z1_w)):
                c[slot, at(i), :] = a[slot, at(i), :] - step * b[slot, at(i), :]
            z1[slot, inner(i), :] = z0[slot, inner(i), :] - step * y1[slot, inner(i), :]
        z1_o[at(i), :] = z0_o[at(i), :] - step * y1_o[at(i), :]
        return 0

    lax.fori_loop(0, strips, blend, 0)
    for slot in (0, 1):
        for lo in (0, HALO + rows):
            z1[slot, lo : lo + 8, :] = z0[slot, lo : lo + 8, :] - step * y1[slot, lo : lo + 8, :]

    def pass2(i, carry):
        (h0, u0), (h1, u1) = couple(z1, z1_e, z1_w, z1_o, i)
        b0 = src[at(i), :]
        r0, r1 = b0 - step * s1[0, at(i), :], -step * s1[1, at(i), :]
        a0, a1 = r0 - u0, r1 - u1
        s2[0, at(i), :] = a0
        s2[1, at(i), :] = a1
        q2[0, at(i), :] = a0 - shift * r0
        q2[1, at(i), :] = a1 - shift * r1
        x0, x1 = solve(i, a0, a1)
        z2[0, inner(i), :] = x0 - shift * h0
        z2[1, inner(i), :] = x1 - shift * h1
        f0, f1 = z0[0, inner(i), :], z0[1, inner(i), :]
        return (
            carry[0] + (f0 * a0 + f1 * a1),
            carry[1] + (h0 * a0 + h1 * a1),
            carry[2] + h0 * b0,
        )

    mids = lax.fori_loop(0, strips, pass2, (zero, zero, zero))
    for c in exchange(z2, z2_e, z2_w, z2_o):
        c.wait()

    def pass3(i, carry):
        (h0, u0), (h1, u1) = couple(z2, z2_e, z2_w, z2_o, i)
        a0, a1 = q2[0, at(i), :] - u0, q2[1, at(i), :] - u1
        s3[0, at(i), :] = a0
        s3[1, at(i), :] = a1
        return (
            carry[0] + (h0 * s1[0, at(i), :] + h1 * s1[1, at(i), :]),
            carry[1] + (h0 * s2[0, at(i), :] + h1 * s2[1, at(i), :]),
            carry[2] + (h0 * a0 + h1 * a1),
            carry[3] + h0 * src[at(i), :],
        )

    lasts = lax.fori_loop(0, strips, pass3, (zero, zero, zero, zero))
    totals = all_sum(1, (*mids, *lasts))
    t01, t11, g1, t02, t12, t22, g2 = [t / mu for t in totals]
    l1, l2 = t01 / shift, t02 / shift
    d1, e1 = t11 - l1 * t01, t12 - l1 * t02
    l3 = e1 / d1
    d2 = t22 - l2 * t02 - l3 * e1
    b1 = g1 - l1
    b2 = g2 - l2 - l3 * b1
    c2 = b2 / d2
    c1 = b1 / d1 - l3 * c2
    c0 = step - l1 * c1 - l2 * c2

    def finish(i, _):
        for slot in (0, 1):
            volt_ref[layer[slot], at(i), :] = (
                c0 * z0[slot, inner(i), :] + c1 * z1[slot, inner(i), :] + c2 * z2[slot, inner(i), :]
            )
            tail = (
                c0 * s1[slot, at(i), :] + c1 * s2[slot, at(i), :] + c2 * s3[slot, at(i), :]
            )
            resid_ref[layer[slot], at(i), :] = (src[at(i), :] - tail) if slot == 0 else -tail
        return 0

    lax.fori_loop(0, strips, finish, 0)


def solution(mesh):
    nx, ny = mesh.shape["gx"], mesh.shape["gy"]

    def shards(load_current, sink_mask, pad_mask, plane_class, via_class, plane_table, via_table):
        _, rows, cols = plane_class.shape
        flat = pltpu.VMEM((rows, cols), F32)
        both = pltpu.VMEM((2, rows, cols), F32)
        tall = pltpu.VMEM((2, rows + 2 * HALO, cols), F32)
        side = pltpu.VMEM((2, rows, LANES), F32)
        side_i = pltpu.VMEM((2, rows, LANES), jnp.int32)
        edge_i = pltpu.VMEM((2, 8, cols), jnp.int32)
        field = [tall, side, side, flat]
        copies = 6 + 3 * 5 + 2 * (nx - 1 + ny - 1 + 1)
        scratch = [
            edge_i, edge_i, side_i, side_i, pltpu.VMEM((rows, cols), jnp.int32),
            pltpu.VMEM(via_table.shape, F32),
            tall, side, side,
            both, both, both, both, flat, flat, flat, flat, flat,
            *field, *field, *field, *field,
            both, both, both, both,
            pltpu.VMEM((2, 3, 1, LANES), F32),
            pltpu.VMEM((2, nx, 1, LANES), F32),
            pltpu.VMEM((2, ny, 1, LANES), F32),
            pltpu.VMEM((2, 2, 1, LANES), F32),
            pltpu.SemaphoreType.DMA((copies,)),
            pltpu.SemaphoreType.DMA((copies,)),
        ]
        shape = jax.ShapeDtypeStruct(plane_class.shape, F32)
        vmem = pl.BlockSpec(memory_space=pltpu.VMEM)
        return pl.pallas_call(
            functools.partial(kernel, (nx, ny, rows, cols)),
            out_shape=(shape, shape),
            in_specs=[vmem] * 7,
            out_specs=(vmem, vmem),
            scratch_shapes=scratch,
            compiler_params=pltpu.CompilerParams(
                collective_id=0, has_side_effects=True, vmem_limit_bytes=56 * 1024 * 1024
            ),
        )(load_current, sink_mask, pad_mask, plane_class, via_class, plane_table, via_table)

    layers = P("gz", "gy", "gx")
    plane = P("gy", "gx")
    table = P("gz", None)
    return jax.shard_map(
        shards,
        mesh=mesh,
        in_specs=(plane, plane, plane, layers, layers, table, table),
        out_specs=(layers, layers),
        check_vma=False,
    )
```

time: 271 us -> 90.8 us (0.34)
  blocking collectives: 158 us -> 0 us
  Pallas kernels: 0 us -> 86.5 us
  starting transfers between devices: 49.4 us -> 0 us
  other arithmetic: 20.9 us -> 0 us
  waiting for transfers between devices: 18.5 us -> 0 us
  between operations: 12 us -> 0.65 us
  local copies, waits for them, and re-layouts: 11.5 us -> 3.02 us
    psum x2 -> x0, blocking collectives: 158 us -> none  [totals(): return lax.psum(jnp.stack([jnp.sum(a * b) for a, b in pairs]), GX_GY_GZ)]
    pallas_call x0 -> x1, Pallas kernels: none -> 86.5 us  [shards(): pl.pallas_call(functools.partial(kernel, (nx, ny, rows, cols)), out_shape...]
    ppermute x24 -> x0, starting transfers between devices: 49.4 us -> none  [the longest x8 22.3 us: padded(): lax.ppermute(leading, axis, [(b, a) for a, b in up])]
    ppermute x24 -> x0, waiting for transfers between devices: 18.5 us -> none  [the longest x4 9.14 us: padded_2(): lax.ppermute(lax.slice_in_dim(block, 0, width, axis=dim), axis, backward)]
    sub x6 -> x0, other arithmetic: 7.04 us -> none  [the longest x1 3.72 us: shards(): residual = s0 - c0 * s1 - c1 * s2 - c2 * s3]
    reduce_sum x2 -> x0, other arithmetic: 6.14 us -> none  [totals(): return lax.psum(jnp.stack([jnp.sum(a * b) for a, b in pairs]), GX_GY_GZ)]
    another operation x3 -> x0, local copies, waits for them, and re-layouts: 5.58 us -> none  [the longest x1 4.35 us: totals(): return lax.psum(jnp.stack([jnp.sum(a * b) for a, b in pairs]), GX_GY_GZ)]
    slice x11 -> x0, local copies, waits for them, and re-layouts: 2.95 us -> none  [the longest x2 1.55 us: lookup(): table[:, level][:, None, None]]
  transfers between devices with their start and end apart: 24 -> 0, of which waited for: 10 -> 0; matrix products, arithmetic and copies ran while one was open for 1% -> 0% of each run, Pallas kernels for 0% -> 0%
where the time goes in v2:
time: 90.8 us; the launch traced here: 90.1 us
  Pallas kernels  86.5 us (95%)
  local copies, waits for them, and re-layouts  3.02 us (3%)
    pallas_call x1, Pallas kernels, shards(): pl.pallas_call(functools.partial(kernel, (nx, ny, rows, cols)), out_shape...  86.5 us
    unnamed x4, local copies, waits for them, and re-layouts  3.02 us

profile of v2, /device:TPU:1, one launch (start us, length us, event | category | flops | bytes accessed | tf_op | source)
XLA Modules:
  0.0 90.1 jit_solution(14993823918342186160)
XLA Ops:
  0.6 86.5 %shard_map.86 = (f32[2,192,512]{2,1,0:T(8,128)}, f32[2,192,512]{2,1,0:T(8,128)}) custom-call(f32[192,512]{1,0:T(8,128)} %load_ref.1, s32[192,512]{1,0:T(8,128)} %sink_ref.1, s32[192,512]{1,0:T(8,128)} %pad_ref.1, s32[2,192,512]{2,1,0:T(8,128)} %plane_ref.1, s32[2,192,512]{2,1,0:T(8,128)} %via_ref.1, f32[2,8]{1,0:T(2,128)} %plane_tab.1, f32[2,8]{1,0:T(2,128)} %via_tab.1), custom_call_target="tpu_custom_call" | custom-call | tf_op jit(solution)/shard_map/pallas_call | solution.py:343
  87.1 0.0 copy-start
  87.1 2.1 %copy.11 = f32[2,192,512]{2,1,0:T(8,128)} copy(f32[2,192,512]{2,1,0:T(8,128)} %get-tuple-element.4) | data formatting | bytes 1572864
  89.3 0.0 copy-done
  89.3 0.9 copy.12
Async XLA Ops:
  87.1 2.1 %copy-start = (f32[2,192,512]{2,1,0:T(8,128)S(1)}, f32[2,192,512]{2,1,0:T(8,128)}, u32[]{:S(2)}) copy-start(f32[2,192,512]{2,1,0:T(8,128)} %get-tuple-element.5) | copy-start | bytes 2359300

commit v3 on v2

v3 whole, which is shorter than its diff:
```python
import functools

import jax
import jax.numpy as jnp
from jax import lax
from jax.experimental import pallas as pl
from jax.experimental.pallas import tpu as pltpu
from jax.sharding import PartitionSpec as P

PAD_CONDUCTANCE = 20.0
MESH = pl.DeviceIdType.MESH
HALO = 8
LANES = 128
CHUNK = 24
F32 = jnp.float32


def harmonic(first, second):
    return 2.0 * first * second / (first + second)


def pick(classes, table):
    low = (classes & 1) == 1
    mid = (classes & 2) == 2
    high = (classes & 4) == 4
    pairs = [jnp.where(low, table[2 * k + 1], table[2 * k]) for k in range(4)]
    return jnp.where(
        high, jnp.where(mid, pairs[3], pairs[2]), jnp.where(mid, pairs[1], pairs[0])
    )


def fold(value):
    return sum(
        value[:, k : k + LANES] for k in range(LANES, value.shape[1], LANES)
    ) + value[:, :LANES]


def kernel(
    sizes,
    load_h, sink_h, pad_h, plane_h, via_h, plane_tab, via_tab,
    volt_h, resid_h,
    load_ref, sink_ref, pad_ref, plane_ref, via_ref, volt_ref, resid_ref,
    via_mine, via_far,
    g_buf, g_e, g_w,
    east, west, north, south, cross, inv0, inv1, mix, src,
    z0, z0_e, z0_w, z0_o, y1, y1_e, y1_w, y1_o, h2, h2_e, h2_w, h2_o, z2, z2_e, z2_w,
    s1, s2, s3,
    part, got_x, got_y, got_z, first_sum,
    in_sem, out_sem, far_send, far_recv, side_send, side_recv, edge_send, edge_recv,
    sum_send, sum_recv,
):
    nx, ny, rows, cols = sizes
    chunks = rows // CHUNK
    per = CHUNK // 8
    ix, iy, iz = lax.axis_index("gx"), lax.axis_index("gy"), lax.axis_index("gz")
    gx_up, gx_dn = lax.rem(ix + 1, nx), lax.rem(ix + nx - 1, nx)
    gy_up, gy_dn = lax.rem(iy + 1, ny), lax.rem(iy + ny - 1, ny)
    other = 1 - iz
    layer = (iz, other)

    fetch = [
        pltpu.make_async_copy(a, b, in_sem.at[k])
        for k, (a, b) in enumerate(
            (
                (via_h, via_ref), (plane_h, plane_ref), (pad_h, pad_ref),
                (sink_h, sink_ref), (load_h, load_ref),
            )
        )
    ]
    for c in fetch:
        c.start()

    barrier = pltpu.get_barrier_semaphore()
    peers = [{"gx": lax.rem(ix + k, nx)} for k in range(1, nx)]
    peers += [{"gy": lax.rem(iy + k, ny)} for k in range(1, ny)]
    peers += [{"gz": other}]
    for peer in peers:
        pl.semaphore_signal(barrier, inc=1, device_id=peer, device_id_type=MESH)
    pl.semaphore_wait(barrier, len(peers))

    def at(c, j=0, n=8):
        return pl.ds(pl.multiple_of(c * CHUNK + 8 * j, 8), n)

    def inner(c, j=0, n=8):
        return pl.ds(pl.multiple_of(c * CHUNK + (8 * j + HALO), 8), n)

    def remote(source, target, send, recv, where_to):
        return pltpu.make_async_remote_copy(
            src_ref=source, dst_ref=target, send_sem=send, recv_sem=recv,
            device_id=where_to, device_id_type=MESH,
        )

    def far_copy(stage, c):
        buf, out = ((via_mine, via_far), (z0, z0_o), (y1, y1_o), (h2, h2_o))[stage]
        source = buf.at[at(c, 0, CHUNK), :] if stage == 0 else buf.at[1, inner(c, 0, CHUNK), :]
        return remote(
            source, out.at[at(c, 0, CHUNK), :],
            far_send.at[stage, c], far_recv.at[stage, c], {"gz": other},
        )

    fields = ((z0, z0_e, z0_w), (y1, y1_e, y1_w), (h2, h2_e, h2_w), (g_buf, g_e, g_w))

    def side_copies(stage, c):
        buf, buf_e, buf_w = fields[stage]
        span = inner(c, 0, CHUNK)
        return [
            remote(
                buf.at[:, span, pl.ds(cols - LANES, LANES)], buf_w.at[:, at(c, 0, CHUNK), :],
                side_send.at[stage, 0, c], side_recv.at[stage, 0, c], {"gx": gx_up},
            ),
            remote(
                buf.at[:, span, pl.ds(0, LANES)], buf_e.at[:, at(c, 0, CHUNK), :],
                side_send.at[stage, 1, c], side_recv.at[stage, 1, c], {"gx": gx_dn},
            ),
        ]

    def edge_copy(stage, way):
        buf = fields[stage][0]
        if way == 0:
            span, out, where_to = pl.ds(rows, 8), pl.ds(0, 8), gy_up
        else:
            span, out, where_to = pl.ds(HALO, 8), pl.ds(HALO + rows, 8), gy_dn
        return remote(
            buf.at[:, span, :], buf.at[:, out, :],
            edge_send.at[stage, way], edge_recv.at[stage, way], {"gy": where_to},
        )

    def send_chunk(stage, c):
        for move in side_copies(stage, c):
            move.start()

        @pl.when(c == chunks - 1)
        def _():
            edge_copy(stage, 0).start()

        @pl.when(c == 0)
        def _():
            edge_copy(stage, 1).start()

    def await_chunk(stage, c):
        for move in side_copies(stage, c):
            move.wait_recv()

        @pl.when(c == 0)
        def _():
            edge_copy(stage, 0).wait_recv()

        @pl.when(c == chunks - 1)
        def _():
            edge_copy(stage, 1).wait_recv()

    def turn(k, shift):
        return lax.rem(k + shift, chunks)

    plane_of = [[plane_tab[layer[slot], k] for k in range(8)] for slot in (0, 1)]
    via_of = [[via_tab[layer[slot], k] for k in range(8)] for slot in (0, 1)]

    fetch[0].wait()

    def lookup_far(k, _):
        c = turn(k, chunks - 1)
        for j in range(per):
            via_mine[at(c, j), :] = pick(via_ref[other, at(c, j), :], via_of[1])
        far_copy(0, c).start()
        return 0

    lax.fori_loop(0, chunks, lookup_far, 0)
    fetch[1].wait()

    def lookup_own(c, _):
        for slot in (0, 1):
            for j in range(per):
                g_buf[slot, inner(c, j), :] = pick(
                    plane_ref[layer[slot], at(c, j), :], plane_of[slot]
                )
        send_chunk(3, c)
        return 0

    lax.fori_loop(0, chunks, lookup_own, 0)

    @pl.when(iz == 0)
    def _():
        def clear(c, _):
            z0_o[at(c, 0, CHUNK), :] = jnp.zeros((CHUNK, cols), F32)
            return 0

        lax.fori_loop(0, chunks, clear, 0)

    for c in fetch[2:]:
        c.wait()

    def around(field, slot, c, j):
        buf, buf_e, buf_w = field
        here = buf[slot, inner(c, j), :]
        below = buf[slot, at(c, j), :]
        above = buf[slot, at(c, j + 2), :]
        up = jnp.concatenate([here[1:], above[:1]], 0)
        down = jnp.concatenate([below[7:], here[:7]], 0)
        right = pltpu.roll(
            jnp.concatenate([here, buf_e[slot, at(c, j), :]], 1), cols + LANES - 1, 1
        )[:, :cols]
        left = pltpu.roll(
            jnp.concatenate([buf_w[slot, at(c, j), :], here], 1), 1, 1
        )[:, LANES:]
        return here, right, left, up, down

    is_source = jnp.where(iz == 0, F32(1.0), F32(0.0))
    pad_scale = jnp.where(iz == 0, F32(0.0), F32(PAD_CONDUCTANCE))

    def solve(span, b0, b1):
        m = mix[span, :]
        x1 = (b1 + m * b0) * inv1[span, :]
        return b0 * inv0[span, :] + m * x1, x1

    def plane_edges(slot, c):
        sums = []
        below = g_buf[slot, at(c), :]
        here = g_buf[slot, inner(c), :]
        last = harmonic(below, jnp.concatenate([below[1:], here[:1]], 0))
        for j in range(per):
            span = at(c, j)
            here = g_buf[slot, inner(c, j), :]
            above = g_buf[slot, at(c, j + 2), :]
            wide = jnp.concatenate([g_w[slot, span, :], here, g_e[slot, span, :]], 1)
            edge = harmonic(wide, pltpu.roll(wide, cols + 2 * LANES - 1, 1))[:, : cols + LANES]
            e = edge[:, LANES:]
            w = pltpu.roll(edge, 1, 1)[:, LANES:]
            n = harmonic(here, jnp.concatenate([here[1:], above[:1]], 0))
            s = jnp.concatenate([last[7:], n[:7]], 0)
            last = n
            east[slot, span, :] = e
            west[slot, span, :] = w
            north[slot, span, :] = n
            south[slot, span, :] = s
            sums.append(e + w + n + s)
        return sums

    def build(k, _):
        c = turn(k, chunks - 1)
        await_chunk(3, c)
        sums = [plane_edges(slot, c) for slot in (0, 1)]
        far_copy(0, c).wait_recv()
        for j in range(per):
            span = at(c, j)
            via0 = pick(via_ref[iz, span, :], via_of[0])
            via1 = via_mine[span, :]
            link = harmonic(via0, via1)
            far = harmonic(via1, via_far[span, :])
            cross[span, :] = far
            d0 = sums[0][j] + link + pad_scale * pad_ref[span, :].astype(F32)
            d1 = sums[1][j] + link + far
            i0 = 1.0 / d0
            m = link * i0
            i1 = 1.0 / (d1 - link * m)
            inv0[span, :] = i0
            inv1[span, :] = i1
            mix[span, :] = m
            b0 = is_source * (sink_ref[span, :].astype(F32) * load_ref[span, :])
            src[span, :] = b0
            x1 = m * b0 * i1
            z0[0, inner(c, j), :] = b0 * i0 + m * x1
            z0[1, inner(c, j), :] = x1

        @pl.when(iz == 0)
        def _():
            far_copy(1, c).start()

        send_chunk(0, c)
        return 0

    lax.fori_loop(0, chunks, build, 0)

    def couple(field, slot, c, j):
        here, right, left, up, down = around(field, slot, c, j)
        span = at(c, j)
        u = (
            east[slot, span, :] * right + west[slot, span, :] * left
            + north[slot, span, :] * up + south[slot, span, :] * down
        )
        return here, u

    zero = jnp.zeros((8, LANES), F32)

    def pass1(k, carry):
        c = turn(k, 0)
        mu, t00 = carry
        await_chunk(0, c)

        @pl.when(iz == 1)
        def _():
            far_copy(1, c).wait_recv()

        for j in range(per):
            span = at(c, j)
            h0, u0 = couple(fields[0], 0, c, j)
            h1, u1 = couple(fields[0], 1, c, j)
            b0 = src[span, :]
            a0, a1 = b0 - u0, -(u1 + cross[span, :] * z0_o[span, :])
            s1[0, span, :] = a0
            s1[1, span, :] = a1
            x0, x1 = solve(span, a0, a1)
            y1[0, inner(c, j), :] = x0
            y1[1, inner(c, j), :] = x1
            mu = mu + fold(h0 * b0)
            t00 = t00 + fold(h0 * a0 + h1 * a1)
        far_copy(2, c).start()
        send_chunk(1, c)
        return mu, t00

    sums = lax.fori_loop(0, chunks, pass1, (zero, zero))

    lane = lax.broadcasted_iota(jnp.int32, (1, LANES), 1)
    axes = (("gx", nx, ix, got_x), ("gy", ny, iy, got_y), ("gz", 2, iz, got_z))
    offset = (0, nx, nx + ny)

    def line_of(values):
        line = jnp.zeros((1, LANES), F32)
        for k, value in enumerate(values):
            line = jnp.where(lane == k, jnp.sum(value), line)
        return line

    def sum_moves(which, stage):
        axis, size, me, got = axes[stage]
        return [
            remote(
                part.at[which, stage], got.at[which, me],
                sum_send.at[which, offset[stage] + k], sum_recv.at[which, offset[stage] + k],
                {axis: lax.rem(me + k, size)},
            )
            for k in range(1, size)
        ]

    def sum_start(which, stage, line):
        part[which, stage] = line
        axes[stage][3][which, axes[stage][2]] = line
        for c in sum_moves(which, stage):
            c.start()

    def sum_finish(which, stage):
        _, size, _, got = axes[stage]
        for c in sum_moves(which, stage):
            c.wait()
        line = got[which, 0]
        for k in range(1, size):
            line = line + got[which, k]
        return line

    def hand_over():
        return remote(
            part.at[0, 2], first_sum, sum_send.at[0, nx + ny], sum_recv.at[0, nx + ny], {"gz": other}
        )

    first_line = line_of(sums)

    @pl.when(iz == 0)
    def _():
        sum_start(0, 0, first_line)

    def pass2(k, _):
        c = turn(k, 1)
        await_chunk(1, c)
        far_copy(2, c).wait_recv()
        for j in range(per):
            span = at(c, j)
            _, u0 = couple(fields[1], 0, c, j)
            _, u1 = couple(fields[1], 1, c, j)
            a0 = s1[0, span, :] - u0
            a1 = s1[1, span, :] - (u1 + cross[span, :] * y1_o[span, :])
            s2[0, span, :] = a0
            s2[1, span, :] = a1
            x0, x1 = solve(span, a0, a1)
            h2[0, inner(c, j), :] = x0
            h2[1, inner(c, j), :] = x1
        far_copy(3, c).start()
        send_chunk(2, c)

        @pl.when(jnp.logical_and(iz == 0, k == chunks // 2))
        def _():
            sum_start(0, 1, sum_finish(0, 0))

        return 0

    lax.fori_loop(0, chunks, pass2, 0)

    @pl.when(iz == 0)
    def _():
        line = sum_finish(0, 1)
        part[0, 2] = line
        first_sum[...] = line
        hand_over().start()
        hand_over().wait_send()

    @pl.when(iz == 1)
    def _():
        hand_over().wait_recv()

    def take(line, k):
        return jnp.sum(jnp.where(lane == k, line, 0.0), axis=1, keepdims=True)

    line = first_sum[...]
    mu, t00 = take(line, 0), take(line, 1)
    step, shift = mu / t00, t00 / mu

    def third(a, b, c):
        return (b - step * c) - shift * (a - step * b)

    def blend(c, _):
        for slot in (0, 1):
            for j in range(per):
                span = inner(c, j)
                z2[slot, span, :] = third(z0[slot, span, :], y1[slot, span, :], h2[slot, span, :])
        return 0

    lax.fori_loop(0, chunks, blend, 0)

    def pass3(k, carry):
        c = jnp.where(k < chunks - 2, k + 1, jnp.where(k == chunks - 2, 0, chunks - 1))
        await_chunk(2, c)

        @pl.when(c == 0)
        def _():
            for slot in (0, 1):
                z2[slot, 0:8, :] = third(z0[slot, 0:8, :], y1[slot, 0:8, :], h2[slot, 0:8, :])

        @pl.when(c == chunks - 1)
        def _():
            top = pl.ds(HALO + rows, 8)
            for slot in (0, 1):
                z2[slot, top, :] = third(z0[slot, top, :], y1[slot, top, :], h2[slot, top, :])

        t01, t11, g1, t02, t12, t22, g2 = carry
        for j in range(per):
            span = at(c, j)
            b0 = src[span, :]
            for slot in (0, 1):
                z2_e[slot, span, :] = third(z0_e[slot, span, :], y1_e[slot, span, :], h2_e[slot, span, :])
                z2_w[slot, span, :] = third(z0_w[slot, span, :], y1_w[slot, span, :], h2_w[slot, span, :])
                h, u = couple((z2, z2_e, z2_w), slot, c, j)
                first = s1[slot, span, :]
                second = first - step * s2[slot, span, :]
                r1 = (b0 - step * first) if slot == 0 else -step * first
                a = (second - shift * r1) - u
                s2[slot, span, :] = second
                s3[slot, span, :] = a
                p = z0[slot, inner(c, j), :]
                q = p - step * y1[slot, inner(c, j), :]
                t01 = t01 + fold(p * second)
                t11 = t11 + fold(q * second)
                t02 = t02 + fold(h * first)
                t12 = t12 + fold(h * second)
                t22 = t22 + fold(h * a)
                if slot == 0:
                    g1 = g1 + fold(q * b0)
                    g2 = g2 + fold(h * b0)
        return t01, t11, g1, t02, t12, t22, g2

    sums = list(lax.fori_loop(0, chunks, pass3, (zero,) * 7))

    def cross_term(k, carry):
        c = turn(k, 1)
        far_copy(3, c).wait_recv()
        for j in range(per):
            span = at(c, j)
            far = cross[span, :] * third(z0_o[span, :], y1_o[span, :], h2_o[span, :])
            s3[1, span, :] = s3[1, span, :] - far
            carry = carry + fold(z2[1, inner(c, j), :] * far)
        return carry

    def far_part():
        return lax.fori_loop(0, chunks, cross_term, zero)

    sums[5] = sums[5] - 2.0 * lax.cond(iz == 0, far_part, lambda: zero)
    line = line_of(sums)
    for stage in range(3):
        sum_start(1, stage, line)
        line = sum_finish(1, stage)

    @pl.when(iz == 1)
    def _():
        far_part()

    t01, t11, g1, t02, t12, t22, g2 = [take(line, k) / mu for k in range(7)]
    l1, l2 = t01 / shift, t02 / shift
    d1, e1 = t11 - l1 * t01, t12 - l1 * t02
    l3 = e1 / d1
    d2 = t22 - l2 * t02 - l3 * e1
    b1 = g1 - l1
    b2 = g2 - l2 - l3 * b1
    c2 = b2 / d2
    c1 = b1 / d1 - l3 * c2
    c0 = step - l1 * c1 - l2 * c2

    def result_copies(c):
        span = at(c, 0, CHUNK)
        return [
            pltpu.make_async_copy(a.at[:, span, :], b.at[:, span, :], out_sem.at[k, c])
            for k, (a, b) in enumerate(((volt_ref, volt_h), (resid_ref, resid_h)))
        ]

    def finish(c, _):
        for slot in (0, 1):
            for j in range(per):
                span, wide = at(c, j), inner(c, j)
                p = z0[slot, wide, :]
                volt_ref[layer[slot], span, :] = (
                    c0 * p + c1 * (p - step * y1[slot, wide, :]) + c2 * z2[slot, wide, :]
                )
                tail = c0 * s1[slot, span, :] + c1 * s2[slot, span, :] + c2 * s3[slot, span, :]
                resid_ref[layer[slot], span, :] = (src[span, :] - tail) if slot == 0 else -tail
        for move in result_copies(c):
            move.start()
        return 0

    lax.fori_loop(0, chunks, finish, 0)

    def drain(c, _):
        for move in result_copies(c):
            move.wait()
        for stage in range(4):
            if stage == 1:

                @pl.when(iz == 0)
                def _():
                    far_copy(1, c).wait_send()

            else:
                far_copy(stage, c).wait_send()
            for move in side_copies(stage, c):
                move.wait_send()
        return 0

    lax.fori_loop(0, chunks, drain, 0)
    for stage in range(4):
        for way in (0, 1):
            edge_copy(stage, way).wait_send()


def solution(mesh):
    nx, ny = mesh.shape["gx"], mesh.shape["gy"]

    def shards(load_current, sink_mask, pad_mask, plane_class, via_class, plane_table, via_table):
        _, rows, cols = plane_class.shape
        chunks = rows // CHUNK
        flat = pltpu.VMEM((rows, cols), F32)
        flat_i = pltpu.VMEM((rows, cols), jnp.int32)
        both = pltpu.VMEM((2, rows, cols), F32)
        both_i = pltpu.VMEM((2, rows, cols), jnp.int32)
        tall = pltpu.VMEM((2, rows + 2 * HALO, cols), F32)
        side = pltpu.VMEM((2, rows, LANES), F32)
        field = [tall, side, side, flat]
        dma = pltpu.SemaphoreType.DMA
        scratch = [
            flat, flat_i, flat_i, both_i, both_i, both, both,
            flat, flat,
            tall, side, side,
            both, both, both, both, flat, flat, flat, flat, flat,
            *field, *field, *field, tall, side, side,
            both, both, both,
            pltpu.VMEM((2, 3, 1, LANES), F32),
            pltpu.VMEM((2, nx, 1, LANES), F32),
            pltpu.VMEM((2, ny, 1, LANES), F32),
            pltpu.VMEM((2, 2, 1, LANES), F32),
            pltpu.VMEM((1, LANES), F32),
            dma((5,)), dma((2, chunks)),
            dma((4, chunks)), dma((4, chunks)),
            dma((4, 2, chunks)), dma((4, 2, chunks)),
            dma((4, 2)), dma((4, 2)),
            dma((2, nx + ny + 2)), dma((2, nx + ny + 2)),
        ]
        shape = jax.ShapeDtypeStruct(plane_class.shape, F32)
        hbm = pl.BlockSpec(memory_space=pl.ANY)
        smem = pl.BlockSpec(memory_space=pltpu.SMEM)
        return pl.pallas_call(
            functools.partial(kernel, (nx, ny, rows, cols)),
            out_shape=(shape, shape),
            in_specs=[hbm] * 5 + [smem] * 2,
            out_specs=(hbm, hbm),
            scratch_shapes=scratch,
            compiler_params=pltpu.CompilerParams(
                collective_id=0, has_side_effects=True, vmem_limit_bytes=48 * 1024 * 1024
            ),
        )(load_current, sink_mask, pad_mask, plane_class, via_class, plane_table, via_table)

    layers = P("gz", "gy", "gx")
    plane = P("gy", "gx")
    table = P("gz", None)
    return jax.shard_map(
        shards,
        mesh=mesh,
        in_specs=(plane, plane, plane, layers, layers, table, table),
        out_specs=(layers, layers),
        check_vma=False,
    )
```

time: 90.8 us -> 80.9 us (0.89)
  the two profiles are of different devices: /device:TPU:1 before, /device:TPU:4 now
where the time goes in v3:
time: 80.9 us; the launch traced here: 80.6 us
  Pallas kernels  71.6 us (89%)
  local copies, waits for them, and re-layouts  8.36 us (10%)
    pallas_call x1, Pallas kernels, shards(): pl.pallas_call(functools.partial(kernel, (nx, ny, rows, cols)), out_shape...  71.6 us
    unnamed x16, local copies, waits for them, and re-layouts  8.36 us

profile of v3, /device:TPU:4, one launch (start us, length us, event | category | flops | bytes accessed | tf_op | source)
XLA Modules:
  0.0 80.6 jit_solution(811975821811545651)
XLA Ops:
  0.6 0.0 copy-start
  0.6 1.1 %copy-done = s32[2,192,512]{2,1,0:T(8,128)S(1)} copy-done((s32[2,192,512]{2,1,0:T(8,128)S(1)}, s32[2,192,512]{2,1,0:T(8,128)}, u32[]{:S(2)}) %copy-start) | copy-done | bytes 786456
  1.8 0.0 copy-start.1
  1.8 1.1 %copy-done.1 = s32[2,192,512]{2,1,0:T(8,128)S(1)} copy-done((s32[2,192,512]{2,1,0:T(8,128)S(1)}, s32[2,192,512]{2,1,0:T(8,128)}, u32[]{:S(2)}) %copy-start.1) | copy-done | bytes 786456
  2.9 0.0 copy-start.2
  2.9 1.0 %copy-done.2 = f32[192,512]{1,0:T(8,128)S(1)} copy-done((f32[192,512]{1,0:T(8,128)S(1)}, f32[192,512]{1,0:T(8,128)}, u32[]{:S(2)}) %copy-start.2) | copy-done | bytes 393240
  3.9 0.0 copy-start.3
  3.9 1.0 %copy-done.3 = s32[192,512]{1,0:T(8,128)S(1)} copy-done((s32[192,512]{1,0:T(8,128)S(1)}, s32[192,512]{1,0:T(8,128)}, u32[]{:S(2)}) %copy-start.3) | copy-done | bytes 393240
  4.9 0.0 copy-start.4
  4.9 1.0 %copy-done.4 = s32[192,512]{1,0:T(8,128)S(1)} copy-done((s32[192,512]{1,0:T(8,128)S(1)}, s32[192,512]{1,0:T(8,128)}, u32[]{:S(2)}) %copy-start.4) | copy-done | bytes 393240
  5.9 0.0 copy-start.5
  5.9 0.7 copy-done.5
  6.6 0.0 copy-start.6
  6.6 0.7 copy-done.6
  7.2 71.6 %shard_map.86 = (f32[2,192,512]{2,1,0:T(8,128)S(1)}, f32[2,192,512]{2,1,0:T(8,128)S(1)}) custom-call(f32[192,512]{1,0:T(8,128)S(1)} %copy-done.2, s32[192,512]{1,0:T(8,128)S(1)} %copy-done.3, s32[192,512]{1,0:T(8,128)S(1)} %copy-done.4, s32[2,192,512]{2,1,0:T(8,128)S(1)} %copy-done, s32[2,192,512]{2,1,0:T(8,128)S(1)} %copy-done.1, f32[2,8]{1,0:T(2,128)S(1)} %copy-done.5, ...), custom_call_target="tpu_custom_call" | custom-call | tf_op jit(solution)/shard_map/pallas_call | solution.py:573
  78.8 0.9 %copy.11 = f32[2,192,512]{2,1,0:T(8,128)} copy(f32[2,192,512]{2,1,0:T(8,128)S(1)} %get-tuple-element.4) | data formatting | bytes 1572864
  79.7 0.9 %copy.12 = f32[2,192,512]{2,1,0:T(8,128)} copy(f32[2,192,512]{2,1,0:T(8,128)S(1)} %get-tuple-element.5) | data formatting | bytes 1572864
Async XLA Ops:
  0.6 1.1 %copy-start = (s32[2,192,512]{2,1,0:T(8,128)S(1)}, s32[2,192,512]{2,1,0:T(8,128)}, u32[]{:S(2)}) copy-start(s32[2,192,512]{2,1,0:T(8,128)} %plane_h.1) | copy-start | bytes 2359300
  1.8 1.1 %copy-start.1 = (s32[2,192,512]{2,1,0:T(8,128)S(1)}, s32[2,192,512]{2,1,0:T(8,128)}, u32[]{:S(2)}) copy-start(s32[2,192,512]{2,1,0:T(8,128)} %via_h.1) | copy-start | bytes 2359300
  2.9 1.0 %copy-start.2 = (f32[192,512]{1,0:T(8,128)S(1)}, f32[192,512]{1,0:T(8,128)}, u32[]{:S(2)}) copy-start(f32[192,512]{1,0:T(8,128)} %load_h.1) | copy-start | bytes 1179652
  3.9 1.0 %copy-start.3 = (s32[192,512]{1,0:T(8,128)S(1)}, s32[192,512]{1,0:T(8,128)}, u32[]{:S(2)}) copy-start(s32[192,512]{1,0:T(8,128)} %sink_h.1) | copy-start | bytes 1179652
  4.9 1.0 %copy-start.4 = (s32[192,512]{1,0:T(8,128)S(1)}, s32[192,512]{1,0:T(8,128)}, u32[]{:S(2)}) copy-start(s32[192,512]{1,0:T(8,128)} %pad_h.1) | copy-start | bytes 1179652
  5.9 0.7 copy-start.5
  6.6 0.7 copy-start.6

commit v4 on v3

--- a/solution.py
+++ b/solution.py
@@ -12,6 +12,8 @@
 HALO = 8
 LANES = 128
 CHUNK = 24
+DEPTH = 2
+AHEAD = 3
 F32 = jnp.float32
 
 
@@ -37,9 +39,9 @@
 
 def kernel(
     sizes,
-    load_h, sink_h, pad_h, plane_h, via_h, plane_tab, via_tab,
+    load_h, sink_h, pad_h, plane_h, via_h, plane_tab_h, via_tab_h,
     volt_h, resid_h,
-    load_ref, sink_ref, pad_ref, plane_ref, via_ref, volt_ref, resid_ref,
+    load_ref, sink_ref, pad_ref, plane_ref, via_ref, plane_tab, via_tab, volt_ref, resid_ref,
     via_mine, via_far,
     g_buf, g_e, g_w,
     east, west, north, south, cross, inv0, inv1, mix, src,
@@ -62,8 +64,8 @@
         pltpu.make_async_copy(a, b, in_sem.at[k])
         for k, (a, b) in enumerate(
             (
-                (via_h, via_ref), (plane_h, plane_ref), (pad_h, pad_ref),
-                (sink_h, sink_ref), (load_h, load_ref),
+                (plane_tab_h, plane_tab), (via_tab_h, via_tab), (plane_h, plane_ref),
+                (via_h, via_ref), (pad_h, pad_ref), (sink_h, sink_ref), (load_h, load_ref),
             )
         )
     ]
@@ -149,25 +151,17 @@
         def _():
             edge_copy(stage, 1).wait_recv()
 
-    def turn(k, shift):
-        return lax.rem(k + shift, chunks)
-
+    def place(k):
+        late = jnp.where(k == 3, chunks - 1, jnp.where(k == 4, 0, k - 1))
+        return jnp.where(k < 3, k + 1, late)
+
+    for c in fetch[:3]:
+        c.wait()
     plane_of = [[plane_tab[layer[slot], k] for k in range(8)] for slot in (0, 1)]
     via_of = [[via_tab[layer[slot], k] for k in range(8)] for slot in (0, 1)]
 
-    fetch[0].wait()
-
-    def lookup_far(k, _):
-        c = turn(k, chunks - 1)
-        for j in range(per):
-            via_mine[at(c, j), :] = pick(via_ref[other, at(c, j), :], via_of[1])
-        far_copy(0, c).start()
-        return 0
-
-    lax.fori_loop(0, chunks, lookup_far, 0)
-    fetch[1].wait()
-
-    def lookup_own(c, _):
+    def lookup_own(k, _):
+        c = place(k)
         for slot in (0, 1):
             for j in range(per):
                 g_buf[slot, inner(c, j), :] = pick(
@@ -177,6 +171,32 @@
         return 0
 
     lax.fori_loop(0, chunks, lookup_own, 0)
+    fetch[3].wait()
+
+    def lookup_far(k, _):
+        c = place(k)
+        for j in range(per):
+            via_mine[at(c, j), :] = pick(via_ref[other, at(c, j), :], via_of[1])
+        far_copy(0, c).start()
+        return 0
+
+    lax.fori_loop(0, chunks, lookup_far, 0)
+
+    def far_step(stage, k):
+        return far_copy(stage, place(k))
+
+    def far_send_next(stage, k):
+        @pl.when(k >= DEPTH)
+        def _():
+            far_step(stage, k - DEPTH).wait_send()
+
+        if stage > 1:
+
+            @pl.when(k < DEPTH)
+            def _():
+                far_step(stage - 1, k + chunks - DEPTH).wait_send()
+
+        far_step(stage, k).start()
 
     @pl.when(iz == 0)
     def _():
@@ -186,7 +206,7 @@
 
         lax.fori_loop(0, chunks, clear, 0)
 
-    for c in fetch[2:]:
+    for c in fetch[4:]:
         c.wait()
 
     def around(field, slot, c, j):
@@ -236,7 +256,7 @@
         return sums
 
     def build(k, _):
-        c = turn(k, chunks - 1)
+        c = place(k)
         await_chunk(3, c)
         sums = [plane_edges(slot, c) for slot in (0, 1)]
         far_copy(0, c).wait_recv()
@@ -261,11 +281,12 @@
             z0[0, inner(c, j), :] = b0 * i0 + m * x1
             z0[1, inner(c, j), :] = x1
 
-        @pl.when(iz == 0)
-        def _():
-            far_copy(1, c).start()
-
         send_chunk(0, c)
+
+        @pl.when(jnp.logical_and(iz == 0, k + AHEAD >= chunks))
+        def _():
+            far_send_next(1, k + AHEAD - chunks)
+
         return 0
 
     lax.fori_loop(0, chunks, build, 0)
@@ -282,7 +303,7 @@
     zero = jnp.zeros((8, LANES), F32)
 
     def pass1(k, carry):
-        c = turn(k, 0)
+        c = place(k)
         mu, t00 = carry
         await_chunk(0, c)
 
@@ -303,8 +324,12 @@
             y1[1, inner(c, j), :] = x1
             mu = mu + fold(h0 * b0)
             t00 = t00 + fold(h0 * a0 + h1 * a1)
-        far_copy(2, c).start()
         send_chunk(1, c)
+
+        @pl.when(iz == 1)
+        def _():
+            far_copy(2, c).start()
+
         return mu, t00
 
     sums = lax.fori_loop(0, chunks, pass1, (zero, zero))
@@ -356,8 +381,15 @@
     def _():
         sum_start(0, 0, first_line)
 
+        def send_rest(k, _):
+            far_send_next(1, k)
+            return 0
+
+        lax.fori_loop(AHEAD, chunks, send_rest, 0)
+        sum_start(0, 1, sum_finish(0, 0))
+
     def pass2(k, _):
-        c = turn(k, 1)
+        c = place(k)
         await_chunk(1, c)
         far_copy(2, c).wait_recv()
         for j in range(per):
@@ -371,12 +403,22 @@
             x0, x1 = solve(span, a0, a1)
             h2[0, inner(c, j), :] = x0
             h2[1, inner(c, j), :] = x1
-        far_copy(3, c).start()
         send_chunk(2, c)
 
+        @pl.when(iz == 1)
+        def _():
+            far_copy(3, c).start()
+
+        @pl.when(iz == 0)
+        def _():
+            far_send_next(2, k)
+
         @pl.when(jnp.logical_and(iz == 0, k == chunks // 2))
         def _():
-            sum_start(0, 1, sum_finish(0, 0))
+            line = sum_finish(0, 1)
+            part[0, 2] = line
+            first_sum[...] = line
+            hand_over().start()
 
         return 0
 
@@ -384,10 +426,6 @@
 
     @pl.when(iz == 0)
     def _():
-        line = sum_finish(0, 1)
-        part[0, 2] = line
-        first_sum[...] = line
-        hand_over().start()
         hand_over().wait_send()
 
     @pl.when(iz == 1)
@@ -414,7 +452,7 @@
     lax.fori_loop(0, chunks, blend, 0)
 
     def pass3(k, carry):
-        c = jnp.where(k < chunks - 2, k + 1, jnp.where(k == chunks - 2, 0, chunks - 1))
+        c = place(k)
         await_chunk(2, c)
 
         @pl.when(c == 0)
@@ -457,13 +495,18 @@
     sums = list(lax.fori_loop(0, chunks, pass3, (zero,) * 7))
 
     def cross_term(k, carry):
-        c = turn(k, 1)
+        c = place(k)
         far_copy(3, c).wait_recv()
         for j in range(per):
             span = at(c, j)
             far = cross[span, :] * third(z0_o[span, :], y1_o[span, :], h2_o[span, :])
             s3[1, span, :] = s3[1, span, :] - far
             carry = carry + fold(z2[1, inner(c, j), :] * far)
+
+        @pl.when(iz == 0)
+        def _():
+            far_send_next(3, k)
+
         return carry
 
     def far_part():
@@ -516,20 +559,25 @@
     def drain(c, _):
         for move in result_copies(c):
             move.wait()
+        far_copy(0, c).wait_send()
+
+        @pl.when(iz == 1)
+        def _():
+            far_copy(2, c).wait_send()
+            far_copy(3, c).wait_send()
+
         for stage in range(4):
-            if stage == 1:
-
-                @pl.when(iz == 0)
-                def _():
-                    far_copy(1, c).wait_send()
-
-            else:
-                far_copy(stage, c).wait_send()
             for move in side_copies(stage, c):
                 move.wait_send()
         return 0
 
     lax.fori_loop(0, chunks, drain, 0)
+
+    @pl.when(iz == 0)
+    def _():
+        for k in range(chunks - DEPTH, chunks):
+            far_step(3, jnp.int32(k)).wait_send()
+
     for stage in range(4):
         for way in (0, 1):
             edge_copy(stage, way).wait_send()
@@ -550,7 +598,8 @@
         field = [tall, side, side, flat]
         dma = pltpu.SemaphoreType.DMA
         scratch = [
-            flat, flat_i, flat_i, both_i, both_i, both, both,
+            flat, flat_i, flat_i, both_i, both_i,
+            pltpu.SMEM(plane_table.shape, F32), pltpu.SMEM(via_table.shape, F32), both, both,
             flat, flat,
             tall, side, side,
             both, both, both, both, flat, flat, flat, flat, flat,
@@ -561,23 +610,23 @@
             pltpu.VMEM((2, ny, 1, LANES), F32),
             pltpu.VMEM((2, 2, 1, LANES), F32),
             pltpu.VMEM((1, LANES), F32),
-            dma((5,)), dma((2, chunks)),
+            dma((7,)), dma((2, chunks)),
             dma((4, chunks)), dma((4, chunks)),
             dma((4, 2, chunks)), dma((4, 2, chunks)),
             dma((4, 2)), dma((4, 2)),
             dma((2, nx + ny + 2)), dma((2, nx + ny + 2)),
         ]
         shape = jax.ShapeDtypeStruct(plane_class.shape, F32)
-        hbm = pl.BlockSpec(memory_space=pl.ANY)
-        smem = pl.BlockSpec(memory_space=pltpu.SMEM)
+        hbm = pl.BlockSpec(memory_space=pltpu.HBM)
+        free = pl.BlockSpec(memory_space=pl.ANY)
         return pl.pallas_call(
             functools.partial(kernel, (nx, ny, rows, cols)),
             out_shape=(shape, shape),
-            in_specs=[hbm] * 5 + [smem] * 2,
-            out_specs=(hbm, hbm),
+            in_specs=[hbm] * 7,
+            out_specs=(free, free),
             scratch_shapes=scratch,
             compiler_params=pltpu.CompilerParams(
-                collective_id=0, has_side_effects=True, vmem_limit_bytes=48 * 1024 * 1024
+                collective_id=0, has_side_effects=True, vmem_limit_bytes=58 * 1024 * 1024
             ),
         )(load_current, sink_mask, pad_mask, plane_class, via_class, plane_table, via_table)
 

time: 80.9 us -> 67.8 us (0.84)
  the two profiles are of different devices: /device:TPU:4 before, /device:TPU:2 now
where the time goes in v4:
time: 67.8 us; the launch traced here: 67.7 us
  Pallas kernels  64.1 us (95%)
  local copies, waits for them, and re-layouts  3.02 us (4%)
    pallas_call x1, Pallas kernels, shards(): pl.pallas_call(functools.partial(kernel, (nx, ny, rows, cols)), out_shape...  64.1 us
    unnamed x4, local copies, waits for them, and re-layouts  3.02 us

profile of v4, /device:TPU:2, one launch (start us, length us, event | category | flops | bytes accessed | tf_op | source)
XLA Modules:
  0.0 67.7 jit_solution(15409226035464926337)
XLA Ops:
  0.6 64.1 %shard_map.86 = (f32[2,192,512]{2,1,0:T(8,128)}, f32[2,192,512]{2,1,0:T(8,128)}) custom-call(f32[192,512]{1,0:T(8,128)} %load_h.1, s32[192,512]{1,0:T(8,128)} %sink_h.1, s32[192,512]{1,0:T(8,128)} %pad_h.1, s32[2,192,512]{2,1,0:T(8,128)} %plane_h.1, s32[2,192,512]{2,1,0:T(8,128)} %via_h.1, f32[2,8]{1,0:T(2,128)} %plane_tab_h.1, f32[2,8]{1,0:T(2,128)} %via_tab_h.1), custom_call_target="tpu_custom_call" | custom-call | tf_op jit(solution)/shard_map/pallas_call | solution.py:622
  64.7 0.0 copy-start
  64.7 2.1 %copy.11 = f32[2,192,512]{2,1,0:T(8,128)} copy(f32[2,192,512]{2,1,0:T(8,128)} %get-tuple-element.4) | data formatting | bytes 1572864
  66.8 0.0 copy-done
  66.8 0.9 %copy.12 = f32[2,192,512]{2,1,0:T(8,128)} copy(f32[2,192,512]{2,1,0:T(8,128)S(1)} %copy-done) | data formatting | bytes 1572864
Async XLA Ops:
  64.7 2.1 %copy-start = (f32[2,192,512]{2,1,0:T(8,128)S(1)}, f32[2,192,512]{2,1,0:T(8,128)}, u32[]{:S(2)}) copy-start(f32[2,192,512]{2,1,0:T(8,128)} %get-tuple-element.5) | copy-start | bytes 2359300

commit v5 on v4

--- a/solution.py
+++ b/solution.py
@@ -12,8 +12,6 @@
 HALO = 8
 LANES = 128
 CHUNK = 24
-DEPTH = 2
-AHEAD = 3
 F32 = jnp.float32
 
 
@@ -47,7 +45,7 @@
     east, west, north, south, cross, inv0, inv1, mix, src,
     z0, z0_e, z0_w, z0_o, y1, y1_e, y1_w, y1_o, h2, h2_e, h2_w, h2_o, z2, z2_e, z2_w,
     s1, s2, s3,
-    part, got_x, got_y, got_z, first_sum,
+    part, got_x, got_y, got_p, first_sum,
     in_sem, out_sem, far_send, far_recv, side_send, side_recv, edge_send, edge_recv,
     sum_send, sum_recv,
 ):
@@ -72,14 +70,15 @@
     for c in fetch:
         c.start()
 
+    def plane_peer(k):
+        there = lax.rem(iy * 2 + iz + k, 2 * ny)
+        return {"gy": there // 2, "gz": lax.rem(there, 2)}
+
     barrier = pltpu.get_barrier_semaphore()
     peers = [{"gx": lax.rem(ix + k, nx)} for k in range(1, nx)]
-    peers += [{"gy": lax.rem(iy + k, ny)} for k in range(1, ny)]
-    peers += [{"gz": other}]
+    peers += [plane_peer(k) for k in range(1, 2 * ny)]
     for peer in peers:
         pl.semaphore_signal(barrier, inc=1, device_id=peer, device_id_type=MESH)
-    pl.semaphore_wait(barrier, len(peers))
-
     def at(c, j=0, n=8):
         return pl.ds(pl.multiple_of(c * CHUNK + 8 * j, 8), n)
 
@@ -151,6 +150,9 @@
         def _():
             edge_copy(stage, 1).wait_recv()
 
+    def turn(k):
+        return lax.rem(k + chunks - 1, chunks)
+
     def place(k):
         late = jnp.where(k == 3, chunks - 1, jnp.where(k == 4, 0, k - 1))
         return jnp.where(k < 3, k + 1, late)
@@ -167,36 +169,52 @@
                 g_buf[slot, inner(c, j), :] = pick(
                     plane_ref[layer[slot], at(c, j), :], plane_of[slot]
                 )
-        send_chunk(3, c)
         return 0
 
     lax.fori_loop(0, chunks, lookup_own, 0)
     fetch[3].wait()
 
     def lookup_far(k, _):
-        c = place(k)
+        c = turn(k)
         for j in range(per):
             via_mine[at(c, j), :] = pick(via_ref[other, at(c, j), :], via_of[1])
-        far_copy(0, c).start()
         return 0
 
     lax.fori_loop(0, chunks, lookup_far, 0)
 
-    def far_step(stage, k):
-        return far_copy(stage, place(k))
-
-    def far_send_next(stage, k):
-        @pl.when(k >= DEPTH)
-        def _():
-            far_step(stage, k - DEPTH).wait_send()
-
-        if stage > 1:
-
-            @pl.when(k < DEPTH)
-            def _():
-                far_step(stage - 1, k + chunks - DEPTH).wait_send()
-
-        far_step(stage, k).start()
+    pl.semaphore_wait(barrier, len(peers))
+
+    def send_edges(k, _):
+        send_chunk(3, turn(k))
+        return 0
+
+    lax.fori_loop(0, chunks, send_edges, 0)
+
+    def far_each(n, stages, act):
+        for stage in stages:
+
+            @pl.when(n // chunks == stage)
+            def _(stage=stage):
+                k = n - stage * chunks
+                act(far_copy(stage, place(k) if stage else turn(k)))
+
+    def far_left(n, stages):
+        far_each(n, stages, lambda move: move.wait_send())
+
+    def far_start(n, stages):
+        far_each(n, stages, lambda move: move.start())
+
+    for n in (0, 1):
+        far_copy(0, turn(jnp.int32(n))).start()
+
+    def lead(n, _):
+        far_left(n - 2, (0,))
+        far_start(n, (0,))
+        return 0
+
+    lax.fori_loop(2, chunks - 2, lead, 0)
+    for n in (chunks - 2, chunks - 1):
+        far_copy(0, turn(jnp.int32(n))).start()
 
     @pl.when(iz == 0)
     def _():
@@ -256,7 +274,7 @@
         return sums
 
     def build(k, _):
-        c = place(k)
+        c = turn(k)
         await_chunk(3, c)
         sums = [plane_edges(slot, c) for slot in (0, 1)]
         far_copy(0, c).wait_recv()
@@ -283,9 +301,10 @@
 
         send_chunk(0, c)
 
-        @pl.when(jnp.logical_and(iz == 0, k + AHEAD >= chunks))
-        def _():
-            far_send_next(1, k + AHEAD - chunks)
+        @pl.when(jnp.logical_and(iz == 0, k >= 4))
+        def _():
+            far_left(k, (0,))
+            far_start(k + 4, (1,))
 
         return 0
 
@@ -305,6 +324,12 @@
     def pass1(k, carry):
         c = place(k)
         mu, t00 = carry
+
+        @pl.when(jnp.logical_and(iz == 0, jnp.logical_or(k == 3, k == 4)))
+        def _():
+            far_left(chunks - 3 + k, (1,))
+            far_start(chunks + 1 + k, (1,))
+
         await_chunk(0, c)
 
         @pl.when(iz == 1)
@@ -335,7 +360,11 @@
     sums = lax.fori_loop(0, chunks, pass1, (zero, zero))
 
     lane = lax.broadcasted_iota(jnp.int32, (1, LANES), 1)
-    axes = (("gx", nx, ix, got_x), ("gy", ny, iy, got_y), ("gz", 2, iz, got_z))
+    rings = (
+        (nx, ix, got_x, lambda k: {"gx": lax.rem(ix + k, nx)}),
+        (ny, iy, got_y, lambda k: {"gy": lax.rem(iy + k, ny)}),
+        (2 * ny, iy * 2 + iz, got_p, plane_peer),
+    )
     offset = (0, nx, nx + ny)
 
     def line_of(values):
@@ -345,24 +374,24 @@
         return line
 
     def sum_moves(which, stage):
-        axis, size, me, got = axes[stage]
+        size, me, got, peer = rings[stage]
         return [
             remote(
                 part.at[which, stage], got.at[which, me],
                 sum_send.at[which, offset[stage] + k], sum_recv.at[which, offset[stage] + k],
-                {axis: lax.rem(me + k, size)},
+                peer(k),
             )
             for k in range(1, size)
         ]
 
     def sum_start(which, stage, line):
         part[which, stage] = line
-        axes[stage][3][which, axes[stage][2]] = line
+        rings[stage][2][which, rings[stage][1]] = line
         for c in sum_moves(which, stage):
             c.start()
 
     def sum_finish(which, stage):
-        _, size, _, got = axes[stage]
+        size, _, got, _ = rings[stage]
         for c in sum_moves(which, stage):
             c.wait()
         line = got[which, 0]
@@ -381,12 +410,9 @@
     def _():
         sum_start(0, 0, first_line)
 
-        def send_rest(k, _):
-            far_send_next(1, k)
-            return 0
-
-        lax.fori_loop(AHEAD, chunks, send_rest, 0)
-        sum_start(0, 1, sum_finish(0, 0))
+        for n in (14, 15, 16):
+            far_left(jnp.int32(n - 4), (1,))
+            far_start(jnp.int32(n), (1, 2))
 
     def pass2(k, _):
         c = place(k)
@@ -411,9 +437,18 @@
 
         @pl.when(iz == 0)
         def _():
-            far_send_next(2, k)
-
-        @pl.when(jnp.logical_and(iz == 0, k == chunks // 2))
+            @pl.when(k == 0)
+            def _():
+                far_left(jnp.int32(13), (1,))
+
+            far_left(14 + k, (1, 2))
+            far_start(17 + k, (2, 3))
+
+        @pl.when(jnp.logical_and(iz == 0, k == 3))
+        def _():
+            sum_start(0, 1, sum_finish(0, 0))
+
+        @pl.when(jnp.logical_and(iz == 0, k == chunks - 1))
         def _():
             line = sum_finish(0, 1)
             part[0, 2] = line
@@ -426,6 +461,11 @@
 
     @pl.when(iz == 0)
     def _():
+        def rest(n, _):
+            far_start(n, (3,))
+            return 0
+
+        lax.fori_loop(25, 4 * chunks, rest, 0)
         hand_over().wait_send()
 
     @pl.when(iz == 1)
@@ -503,10 +543,6 @@
             s3[1, span, :] = s3[1, span, :] - far
             carry = carry + fold(z2[1, inner(c, j), :] * far)
 
-        @pl.when(iz == 0)
-        def _():
-            far_send_next(3, k)
-
         return carry
 
     def far_part():
@@ -514,7 +550,7 @@
 
     sums[5] = sums[5] - 2.0 * lax.cond(iz == 0, far_part, lambda: zero)
     line = line_of(sums)
-    for stage in range(3):
+    for stage in (0, 2):
         sum_start(1, stage, line)
         line = sum_finish(1, stage)
 
@@ -559,8 +595,6 @@
     def drain(c, _):
         for move in result_copies(c):
             move.wait()
-        far_copy(0, c).wait_send()
-
         @pl.when(iz == 1)
         def _():
             far_copy(2, c).wait_send()
@@ -575,8 +609,15 @@
 
     @pl.when(iz == 0)
     def _():
-        for k in range(chunks - DEPTH, chunks):
-            far_step(3, jnp.int32(k)).wait_send()
+        for n in (22, 23):
+            far_left(jnp.int32(n), (2,))
+        for k in range(chunks):
+            far_copy(3, place(jnp.int32(k))).wait_send()
+
+    @pl.when(iz == 1)
+    def _():
+        for k in range(4, chunks):
+            far_copy(0, turn(jnp.int32(k))).wait_send()
 
     for stage in range(4):
         for way in (0, 1):
@@ -608,13 +649,13 @@
             pltpu.VMEM((2, 3, 1, LANES), F32),
             pltpu.VMEM((2, nx, 1, LANES), F32),
             pltpu.VMEM((2, ny, 1, LANES), F32),
-            pltpu.VMEM((2, 2, 1, LANES), F32),
+            pltpu.VMEM((2, 2 * ny, 1, LANES), F32),
             pltpu.VMEM((1, LANES), F32),
             dma((7,)), dma((2, chunks)),
             dma((4, chunks)), dma((4, chunks)),
             dma((4, 2, chunks)), dma((4, 2, chunks)),
             dma((4, 2)), dma((4, 2)),
-            dma((2, nx + ny + 2)), dma((2, nx + ny + 2)),
+            dma((2, nx + 3 * ny)), dma((2, nx + 3 * ny)),
         ]
         shape = jax.ShapeDtypeStruct(plane_class.shape, F32)
         hbm = pl.BlockSpec(memory_space=pltpu.HBM)

time: 67.8 us -> 61.3 us (0.904)
  the two profiles are of different devices: /device:TPU:2 before, /device:TPU:1 now
where the time goes in v5:
time: 61.3 us; the launch traced here: 61.2 us
  Pallas kernels  57.5 us (94%)
  local copies, waits for them, and re-layouts  3.02 us (5%)
  between operations  0.65 us (1%)
    pallas_call x1, Pallas kernels, shards(): pl.pallas_call(functools.partial(kernel, (nx, ny, rows, cols)), out_shape...  57.5 us
    unnamed x4, local copies, waits for them, and re-layouts  3.02 us

profile of v5, /device:TPU:1, one launch (start us, length us, event | category | flops | bytes accessed | tf_op | source)
XLA Modules:
  0.0 61.2 jit_solution(9973006144821431349)
XLA Ops:
  0.6 57.5 %shard_map.86 = (f32[2,192,512]{2,1,0:T(8,128)}, f32[2,192,512]{2,1,0:T(8,128)}) custom-call(f32[192,512]{1,0:T(8,128)} %load_h.1, s32[192,512]{1,0:T(8,128)} %sink_h.1, s32[192,512]{1,0:T(8,128)} %pad_h.1, s32[2,192,512]{2,1,0:T(8,128)} %plane_h.1, s32[2,192,512]{2,1,0:T(8,128)} %via_h.1, f32[2,8]{1,0:T(2,128)} %plane_tab_h.1, f32[2,8]{1,0:T(2,128)} %via_tab_h.1), custom_call_target="tpu_custom_call" | custom-call | tf_op jit(solution)/shard_map/pallas_call | solution.py:663
  58.2 0.0 copy-start
  58.2 2.1 %copy.11 = f32[2,192,512]{2,1,0:T(8,128)} copy(f32[2,192,512]{2,1,0:T(8,128)} %get-tuple-element.4) | data formatting | bytes 1572864
  60.3 0.0 copy-done
  60.3 0.9 %copy.12 = f32[2,192,512]{2,1,0:T(8,128)} copy(f32[2,192,512]{2,1,0:T(8,128)S(1)} %copy-done) | data formatting | bytes 1572864
Async XLA Ops:
  58.2 2.1 %copy-start = (f32[2,192,512]{2,1,0:T(8,128)S(1)}, f32[2,192,512]{2,1,0:T(8,128)}, u32[]{:S(2)}) copy-start(f32[2,192,512]{2,1,0:T(8,128)} %get-tuple-element.5) | copy-start | bytes 2359300

commit v6 on v5

--- a/solution.py
+++ b/solution.py
@@ -38,15 +38,15 @@
 def kernel(
     sizes,
     load_h, sink_h, pad_h, plane_h, via_h, plane_tab_h, via_tab_h,
-    volt_h, resid_h,
-    load_ref, sink_ref, pad_ref, plane_ref, via_ref, plane_tab, via_tab, volt_ref, resid_ref,
+    volt_ref, resid_ref,
+    load_ref, sink_ref, pad_ref, plane_ref, via_ref, plane_tab, via_tab,
     via_mine, via_far,
     g_buf, g_e, g_w,
     east, west, north, south, cross, inv0, inv1, mix, src,
     z0, z0_e, z0_w, z0_o, y1, y1_e, y1_w, y1_o, h2, h2_e, h2_w, h2_o, z2, z2_e, z2_w,
     s1, s2, s3,
     part, got_x, got_y, got_p, first_sum,
-    in_sem, out_sem, far_send, far_recv, side_send, side_recv, edge_send, edge_recv,
+    in_sem, far_send, far_recv, side_send, side_recv, edge_send, edge_recv,
     sum_send, sum_recv,
 ):
     nx, ny, rows, cols = sizes
@@ -107,11 +107,11 @@
         return [
             remote(
                 buf.at[:, span, pl.ds(cols - LANES, LANES)], buf_w.at[:, at(c, 0, CHUNK), :],
-                side_send.at[stage, 0, c], side_recv.at[stage, 0, c], {"gx": gx_up},
+                side_send.at[stage, 0], side_recv.at[stage, c], {"gx": gx_up},
             ),
             remote(
                 buf.at[:, span, pl.ds(0, LANES)], buf_e.at[:, at(c, 0, CHUNK), :],
-                side_send.at[stage, 1, c], side_recv.at[stage, 1, c], {"gx": gx_dn},
+                side_send.at[stage, 1], side_recv.at[stage, c], {"gx": gx_dn},
             ),
         ]
 
@@ -139,8 +139,8 @@
             edge_copy(stage, 1).start()
 
     def await_chunk(stage, c):
-        for move in side_copies(stage, c):
-            move.wait_recv()
+        both = fields[stage][0].at[:, inner(c, 0, CHUNK), pl.ds(0, 2 * LANES)]
+        remote(both, both, side_send.at[stage, 0], side_recv.at[stage, c], {"gx": gx_up}).wait_recv()
 
         @pl.when(c == 0)
         def _():
@@ -365,7 +365,6 @@
         (ny, iy, got_y, lambda k: {"gy": lax.rem(iy + k, ny)}),
         (2 * ny, iy * 2 + iz, got_p, plane_peer),
     )
-    offset = (0, nx, nx + ny)
 
     def line_of(values):
         line = jnp.zeros((1, LANES), F32)
@@ -378,7 +377,7 @@
         return [
             remote(
                 part.at[which, stage], got.at[which, me],
-                sum_send.at[which, offset[stage] + k], sum_recv.at[which, offset[stage] + k],
+                sum_send.at[which, stage], sum_recv.at[which, stage],
                 peer(k),
             )
             for k in range(1, size)
@@ -391,9 +390,11 @@
             c.start()
 
     def sum_finish(which, stage):
-        size, _, got, _ = rings[stage]
-        for c in sum_moves(which, stage):
-            c.wait()
+        size, _, got, peer = rings[stage]
+        all_in = got.at[which, pl.ds(0, size - 1)]
+        whole = remote(all_in, all_in, sum_send.at[which, stage], sum_recv.at[which, stage], peer(1))
+        whole.wait_recv()
+        whole.wait_send()
         line = got[which, 0]
         for k in range(1, size):
             line = line + got[which, k]
@@ -401,7 +402,7 @@
 
     def hand_over():
         return remote(
-            part.at[0, 2], first_sum, sum_send.at[0, nx + ny], sum_recv.at[0, nx + ny], {"gz": other}
+            part.at[0, 2], first_sum, sum_send.at[0, 2], sum_recv.at[0, 2], {"gz": other}
         )
 
     first_line = line_of(sums)
@@ -569,13 +570,6 @@
     c1 = b1 / d1 - l3 * c2
     c0 = step - l1 * c1 - l2 * c2
 
-    def result_copies(c):
-        span = at(c, 0, CHUNK)
-        return [
-            pltpu.make_async_copy(a.at[:, span, :], b.at[:, span, :], out_sem.at[k, c])
-            for k, (a, b) in enumerate(((volt_ref, volt_h), (resid_ref, resid_h)))
-        ]
-
     def finish(c, _):
         for slot in (0, 1):
             for j in range(per):
@@ -586,23 +580,16 @@
                 )
                 tail = c0 * s1[slot, span, :] + c1 * s2[slot, span, :] + c2 * s3[slot, span, :]
                 resid_ref[layer[slot], span, :] = (src[span, :] - tail) if slot == 0 else -tail
-        for move in result_copies(c):
-            move.start()
         return 0
 
     lax.fori_loop(0, chunks, finish, 0)
 
     def drain(c, _):
-        for move in result_copies(c):
-            move.wait()
         @pl.when(iz == 1)
         def _():
             far_copy(2, c).wait_send()
             far_copy(3, c).wait_send()
 
-        for stage in range(4):
-            for move in side_copies(stage, c):
-                move.wait_send()
         return 0
 
     lax.fori_loop(0, chunks, drain, 0)
@@ -620,8 +607,12 @@
             far_copy(0, turn(jnp.int32(k))).wait_send()
 
     for stage in range(4):
+        _, buf_e, buf_w = fields[stage]
         for way in (0, 1):
             edge_copy(stage, way).wait_send()
+            remote(
+                buf_e, buf_w, side_send.at[stage, way], side_recv.at[stage, 0], {"gx": gx_up}
+            ).wait_send()
 
 
 def solution(mesh):
@@ -640,7 +631,7 @@
         dma = pltpu.SemaphoreType.DMA
         scratch = [
             flat, flat_i, flat_i, both_i, both_i,
-            pltpu.SMEM(plane_table.shape, F32), pltpu.SMEM(via_table.shape, F32), both, both,
+            pltpu.SMEM(plane_table.shape, F32), pltpu.SMEM(via_table.shape, F32),
             flat, flat,
             tall, side, side,
             both, both, both, both, flat, flat, flat, flat, flat,
@@ -651,25 +642,29 @@
             pltpu.VMEM((2, ny, 1, LANES), F32),
             pltpu.VMEM((2, 2 * ny, 1, LANES), F32),
             pltpu.VMEM((1, LANES), F32),
-            dma((7,)), dma((2, chunks)),
+            dma((7,)),
             dma((4, chunks)), dma((4, chunks)),
-            dma((4, 2, chunks)), dma((4, 2, chunks)),
+            dma((4, 2)), dma((4, chunks)),
             dma((4, 2)), dma((4, 2)),
-            dma((2, nx + 3 * ny)), dma((2, nx + 3 * ny)),
+            dma((2, 3)), dma((2, 3)),
         ]
-        shape = jax.ShapeDtypeStruct(plane_class.shape, F32)
+        shape = pltpu.VMEM(plane_class.shape, F32)
         hbm = pl.BlockSpec(memory_space=pltpu.HBM)
-        free = pl.BlockSpec(memory_space=pl.ANY)
+        vmem = pl.BlockSpec(memory_space=pltpu.VMEM)
+        held = [
+            pltpu.with_memory_space_constraint(a, pltpu.HBM)
+            for a in (load_current, sink_mask, pad_mask, plane_class, via_class, plane_table, via_table)
+        ]
         return pl.pallas_call(
             functools.partial(kernel, (nx, ny, rows, cols)),
             out_shape=(shape, shape),
             in_specs=[hbm] * 7,
-            out_specs=(free, free),
+            out_specs=(vmem, vmem),
             scratch_shapes=scratch,
             compiler_params=pltpu.CompilerParams(
-                collective_id=0, has_side_effects=True, vmem_limit_bytes=58 * 1024 * 1024
+                collective_id=0, has_side_effects=True, vmem_limit_bytes=48 * 1024 * 1024
             ),
-        )(load_current, sink_mask, pad_mask, plane_class, via_class, plane_table, via_table)
+        )(*held)
 
     layers = P("gz", "gy", "gx")
     plane = P("gy", "gx")

time: 61.3 us -> 57 us (0.930)
  Pallas kernels: 57.5 us -> 54.5 us
  local copies, waits for them, and re-layouts: 3.02 us -> 1.76 us
    pallas_call x1, Pallas kernels: 57.5 us -> 54.5 us  [shards(): pl.pallas_call(functools.partial(kernel, (nx, ny, rows, cols)), out_shape...]
    unnamed x4 -> x2, local copies, waits for them, and re-layouts: 3.02 us -> 1.76 us
where the time goes in v6:
time: 57 us; the launch traced here: 56.9 us
  Pallas kernels  54.5 us (96%)
  local copies, waits for them, and re-layouts  1.76 us (3%)
  between operations  0.64 us (1%)
    pallas_call x1, Pallas kernels, shards(): pl.pallas_call(functools.partial(kernel, (nx, ny, rows, cols)), out_shape...  54.5 us
    unnamed x2, local copies, waits for them, and re-layouts  1.76 us

profile of v6, /device:TPU:1, one launch (start us, length us, event | category | flops | bytes accessed | tf_op | source)
XLA Modules:
  0.0 56.9 jit_solution(14212706605276341815)
XLA Ops:
  0.6 54.5 %shard_map.86 = (f32[2,192,512]{2,1,0:T(8,128)S(1)}, f32[2,192,512]{2,1,0:T(8,128)S(1)}) custom-call(f32[192,512]{1,0:T(8,128)} %load_h.1, s32[192,512]{1,0:T(8,128)} %sink_h.1, s32[192,512]{1,0:T(8,128)} %pad_h.1, s32[2,192,512]{2,1,0:T(8,128)} %plane_h.1, s32[2,192,512]{2,1,0:T(8,128)} %via_h.1, f32[2,8]{1,0:T(2,128)} %plane_tab_h.1, f32[2,8]{1,0:T(2,128)} %via_tab_h.1), custom_call_target="tpu_custom_call" | custom-call | tf_op jit(solution)/shard_map/pallas_call | solution.py:658
  55.1 0.9 %copy.11 = f32[2,192,512]{2,1,0:T(8,128)} copy(f32[2,192,512]{2,1,0:T(8,128)S(1)} %get-tuple-element.2) | data formatting | bytes 1572864
  56.0 0.9 %copy.12 = f32[2,192,512]{2,1,0:T(8,128)} copy(f32[2,192,512]{2,1,0:T(8,128)S(1)} %get-tuple-element.3) | data formatting | bytes 1572864

commit v7 on v6

--- a/solution.py
+++ b/solution.py
@@ -45,7 +45,7 @@
     east, west, north, south, cross, inv0, inv1, mix, src,
     z0, z0_e, z0_w, z0_o, y1, y1_e, y1_w, y1_o, h2, h2_e, h2_w, h2_o, z2, z2_e, z2_w,
     s1, s2, s3,
-    part, got_x, got_y, got_p, first_sum,
+    edge_out, edge_in, part, got_x, got_p,
     in_sem, far_send, far_recv, side_send, side_recv, edge_send, edge_recv,
     sum_send, sum_recv,
 ):
@@ -116,15 +116,28 @@
         ]
 
     def edge_copy(stage, way):
-        buf = fields[stage][0]
-        if way == 0:
-            span, out, where_to = pl.ds(rows, 8), pl.ds(0, 8), gy_up
-        else:
-            span, out, where_to = pl.ds(HALO, 8), pl.ds(HALO + rows, 8), gy_dn
         return remote(
-            buf.at[:, span, :], buf.at[:, out, :],
-            edge_send.at[stage, way], edge_recv.at[stage, way], {"gy": where_to},
+            edge_out.at[stage, way], edge_in.at[stage, way],
+            edge_send.at[stage, way], edge_recv.at[stage, way], {"gy": (gy_up, gy_dn)[way]},
         )
+
+    parts = [
+        (slot, slot * (cols // LANES) + b, slice(b * LANES, (b + 1) * LANES))
+        for slot in (0, 1)
+        for b in range(cols // LANES)
+    ]
+
+    def edge_start(stage, way):
+        row = (HALO + rows - 1, HALO)[way]
+        for slot, k, lanes in parts:
+            edge_out[stage, way, k : k + 1, :] = fields[stage][0][slot, row : row + 1, lanes]
+        edge_copy(stage, way).start()
+
+    def edge_finish(stage, way):
+        edge_copy(stage, way).wait_recv()
+        row = (HALO - 1, HALO + rows)[way]
+        for slot, k, lanes in parts:
+            fields[stage][0][slot, row : row + 1, lanes] = edge_in[stage, way, k : k + 1, :]
 
     def send_chunk(stage, c):
         for move in side_copies(stage, c):
@@ -132,11 +145,11 @@
 
         @pl.when(c == chunks - 1)
         def _():
-            edge_copy(stage, 0).start()
+            edge_start(stage, 0)
 
         @pl.when(c == 0)
         def _():
-            edge_copy(stage, 1).start()
+            edge_start(stage, 1)
 
     def await_chunk(stage, c):
         both = fields[stage][0].at[:, inner(c, 0, CHUNK), pl.ds(0, 2 * LANES)]
@@ -144,11 +157,11 @@
 
         @pl.when(c == 0)
         def _():
-            edge_copy(stage, 0).wait_recv()
+            edge_finish(stage, 0)
 
         @pl.when(c == chunks - 1)
         def _():
-            edge_copy(stage, 1).wait_recv()
+            edge_finish(stage, 1)
 
     def turn(k):
         return lax.rem(k + chunks - 1, chunks)
@@ -362,7 +375,6 @@
     lane = lax.broadcasted_iota(jnp.int32, (1, LANES), 1)
     rings = (
         (nx, ix, got_x, lambda k: {"gx": lax.rem(ix + k, nx)}),
-        (ny, iy, got_y, lambda k: {"gy": lax.rem(iy + k, ny)}),
         (2 * ny, iy * 2 + iz, got_p, plane_peer),
     )
 
@@ -399,11 +411,6 @@
         for k in range(1, size):
             line = line + got[which, k]
         return line
-
-    def hand_over():
-        return remote(
-            part.at[0, 2], first_sum, sum_send.at[0, 2], sum_recv.at[0, 2], {"gz": other}
-        )
 
     first_line = line_of(sums)
 
@@ -445,38 +452,39 @@
             far_left(14 + k, (1, 2))
             far_start(17 + k, (2, 3))
 
-        @pl.when(jnp.logical_and(iz == 0, k == 3))
+        @pl.when(jnp.logical_and(iz == 0, k == 2))
         def _():
             sum_start(0, 1, sum_finish(0, 0))
 
-        @pl.when(jnp.logical_and(iz == 0, k == chunks - 1))
-        def _():
-            line = sum_finish(0, 1)
-            part[0, 2] = line
-            first_sum[...] = line
-            hand_over().start()
-
         return 0
 
     lax.fori_loop(0, chunks, pass2, 0)
+
+    def plane_arrived(count):
+        all_in = got_p.at[0, pl.ds(0, count)]
+        return remote(all_in, all_in, sum_send.at[0, 1], sum_recv.at[0, 1], plane_peer(1))
 
     @pl.when(iz == 0)
     def _():
+        plane_arrived(ny - 1).wait_recv()
+        plane_arrived(2 * ny - 1).wait_send()
+
         def rest(n, _):
             far_start(n, (3,))
             return 0
 
         lax.fori_loop(25, 4 * chunks, rest, 0)
-        hand_over().wait_send()
 
     @pl.when(iz == 1)
     def _():
-        hand_over().wait_recv()
+        plane_arrived(ny).wait_recv()
 
     def take(line, k):
         return jnp.sum(jnp.where(lane == k, line, 0.0), axis=1, keepdims=True)
 
-    line = first_sum[...]
+    line = got_p[0, 0]
+    for k in range(1, ny):
+        line = line + got_p[0, 2 * k]
     mu, t00 = take(line, 0), take(line, 1)
     step, shift = mu / t00, t00 / mu
 
@@ -493,7 +501,7 @@
     lax.fori_loop(0, chunks, blend, 0)
 
     def pass3(k, carry):
-        c = place(k)
+        c = lax.rem(k + 1, chunks)
         await_chunk(2, c)
 
         @pl.when(c == 0)
@@ -551,7 +559,7 @@
 
     sums[5] = sums[5] - 2.0 * lax.cond(iz == 0, far_part, lambda: zero)
     line = line_of(sums)
-    for stage in (0, 2):
+    for stage in (0, 1):
         sum_start(1, stage, line)
         line = sum_finish(1, stage)
 
@@ -637,16 +645,16 @@
             both, both, both, both, flat, flat, flat, flat, flat,
             *field, *field, *field, tall, side, side,
             both, both, both,
-            pltpu.VMEM((2, 3, 1, LANES), F32),
+            pltpu.VMEM((4, 2, 2 * cols // LANES, LANES), F32),
+            pltpu.VMEM((4, 2, 2 * cols // LANES, LANES), F32),
+            pltpu.VMEM((2, 2, 1, LANES), F32),
             pltpu.VMEM((2, nx, 1, LANES), F32),
-            pltpu.VMEM((2, ny, 1, LANES), F32),
             pltpu.VMEM((2, 2 * ny, 1, LANES), F32),
-            pltpu.VMEM((1, LANES), F32),
             dma((7,)),
             dma((4, chunks)), dma((4, chunks)),
             dma((4, 2)), dma((4, chunks)),
             dma((4, 2)), dma((4, 2)),
-            dma((2, 3)), dma((2, 3)),
+            dma((2, 2)), dma((2, 2)),
         ]
         shape = pltpu.VMEM(plane_class.shape, F32)
         hbm = pl.BlockSpec(memory_space=pltpu.HBM)

time: 57 us -> 54.6 us (0.958)
  Pallas kernels: 54.5 us -> 52.1 us
    pallas_call x1, Pallas kernels: 54.5 us -> 52.1 us  [shards(): pl.pallas_call(functools.partial(kernel, (nx, ny, rows, cols)), out_shape...]
where the time goes in v7:
time: 54.6 us; the launch traced here: 54.5 us
  Pallas kernels  52.1 us (95%)
  local copies, waits for them, and re-layouts  1.76 us (3%)
  between operations  0.64 us (1%)
    pallas_call x1, Pallas kernels, shards(): pl.pallas_call(functools.partial(kernel, (nx, ny, rows, cols)), out_shape...  52.1 us
    unnamed x2, local copies, waits for them, and re-layouts  1.76 us

profile of v7, /device:TPU:1, one launch (start us, length us, event | category | flops | bytes accessed | tf_op | source)
XLA Modules:
  0.0 54.5 jit_solution(14664820798186206367)
XLA Ops:
  0.6 52.1 %shard_map.86 = (f32[2,192,512]{2,1,0:T(8,128)S(1)}, f32[2,192,512]{2,1,0:T(8,128)S(1)}) custom-call(f32[192,512]{1,0:T(8,128)} %load_h.1, s32[192,512]{1,0:T(8,128)} %sink_h.1, s32[192,512]{1,0:T(8,128)} %pad_h.1, s32[2,192,512]{2,1,0:T(8,128)} %plane_h.1, s32[2,192,512]{2,1,0:T(8,128)} %via_h.1, f32[2,8]{1,0:T(2,128)} %plane_tab_h.1, f32[2,8]{1,0:T(2,128)} %via_tab_h.1), custom_call_target="tpu_custom_call" | custom-call | tf_op jit(solution)/shard_map/pallas_call | solution.py:666
  52.8 0.9 %copy.11 = f32[2,192,512]{2,1,0:T(8,128)} copy(f32[2,192,512]{2,1,0:T(8,128)S(1)} %get-tuple-element.2) | data formatting | bytes 1572864
  53.7 0.9 %copy.12 = f32[2,192,512]{2,1,0:T(8,128)} copy(f32[2,192,512]{2,1,0:T(8,128)S(1)} %get-tuple-element.3) | data formatting | bytes 1572864

commit v8 on v7

--- a/solution.py
+++ b/solution.py
@@ -62,8 +62,8 @@
         pltpu.make_async_copy(a, b, in_sem.at[k])
         for k, (a, b) in enumerate(
             (
-                (plane_tab_h, plane_tab), (via_tab_h, via_tab), (plane_h, plane_ref),
-                (via_h, via_ref), (pad_h, pad_ref), (sink_h, sink_ref), (load_h, load_ref),
+                (via_tab_h, via_tab), (via_h.at[other], via_ref.at[other]), (plane_tab_h, plane_tab),
+                (plane_h, plane_ref), (via_h.at[iz], via_ref.at[iz]), (pad_h, pad_ref), (sink_h, sink_ref), (load_h, load_ref),
             )
         )
     ]
@@ -170,38 +170,36 @@
         late = jnp.where(k == 3, chunks - 1, jnp.where(k == 4, 0, k - 1))
         return jnp.where(k < 3, k + 1, late)
 
-    for c in fetch[:3]:
+    for c in fetch[:2]:
+        c.wait()
+    via_of = [[via_tab[layer[slot], k] for k in range(8)] for slot in (0, 1)]
+
+    def lookup_far(k, _):
+        c = turn(k)
+        for j in range(per):
+            via_mine[at(c, j), :] = pick(via_ref[other, at(c, j), :], via_of[1])
+        return 0
+
+    lax.fori_loop(0, chunks, lookup_far, 0)
+    pl.semaphore_wait(barrier, len(peers))
+    for n in (0, 1):
+        far_copy(0, turn(jnp.int32(n))).start()
+
+    for c in fetch[2:4]:
         c.wait()
     plane_of = [[plane_tab[layer[slot], k] for k in range(8)] for slot in (0, 1)]
-    via_of = [[via_tab[layer[slot], k] for k in range(8)] for slot in (0, 1)]
 
     def lookup_own(k, _):
-        c = place(k)
+        c = turn(k)
         for slot in (0, 1):
             for j in range(per):
                 g_buf[slot, inner(c, j), :] = pick(
                     plane_ref[layer[slot], at(c, j), :], plane_of[slot]
                 )
+        send_chunk(3, c)
         return 0
 
     lax.fori_loop(0, chunks, lookup_own, 0)
-    fetch[3].wait()
-
-    def lookup_far(k, _):
-        c = turn(k)
-        for j in range(per):
-            via_mine[at(c, j), :] = pick(via_ref[other, at(c, j), :], via_of[1])
-        return 0
-
-    lax.fori_loop(0, chunks, lookup_far, 0)
-
-    pl.semaphore_wait(barrier, len(peers))
-
-    def send_edges(k, _):
-        send_chunk(3, turn(k))
-        return 0
-
-    lax.fori_loop(0, chunks, send_edges, 0)
 
     def far_each(n, stages, act):
         for stage in stages:
@@ -216,9 +214,6 @@
 
     def far_start(n, stages):
         far_each(n, stages, lambda move: move.start())
-
-    for n in (0, 1):
-        far_copy(0, turn(jnp.int32(n))).start()
 
     def lead(n, _):
         far_left(n - 2, (0,))
@@ -443,14 +438,14 @@
         def _():
             far_copy(3, c).start()
 
-        @pl.when(iz == 0)
+        @pl.when(jnp.logical_and(iz == 0, k < chunks - 1))
         def _():
             @pl.when(k == 0)
             def _():
                 far_left(jnp.int32(13), (1,))
 
             far_left(14 + k, (1, 2))
-            far_start(17 + k, (2, 3))
+            far_start(17 + k, (2,))
 
         @pl.when(jnp.logical_and(iz == 0, k == 2))
         def _():
@@ -459,6 +454,13 @@
         return 0
 
     lax.fori_loop(0, chunks, pass2, 0)
+
+    def send_rest(first, last):
+        def rest(n, _):
+            far_start(n, (3,))
+            return 0
+
+        lax.fori_loop(first, last, rest, 0)
 
     def plane_arrived(count):
         all_in = got_p.at[0, pl.ds(0, count)]
@@ -468,12 +470,6 @@
     def _():
         plane_arrived(ny - 1).wait_recv()
         plane_arrived(2 * ny - 1).wait_send()
-
-        def rest(n, _):
-            far_start(n, (3,))
-            return 0
-
-        lax.fori_loop(25, 4 * chunks, rest, 0)
 
     @pl.when(iz == 1)
     def _():
@@ -543,6 +539,10 @@
 
     sums = list(lax.fori_loop(0, chunks, pass3, (zero,) * 7))
 
+    @pl.when(iz == 0)
+    def _():
+        send_rest(24, 32)
+
     def cross_term(k, carry):
         c = place(k)
         far_copy(3, c).wait_recv()
@@ -558,6 +558,7 @@
         return lax.fori_loop(0, chunks, cross_term, zero)
 
     sums[5] = sums[5] - 2.0 * lax.cond(iz == 0, far_part, lambda: zero)
+
     line = line_of(sums)
     for stage in (0, 1):
         sum_start(1, stage, line)
@@ -604,7 +605,7 @@
 
     @pl.when(iz == 0)
     def _():
-        for n in (22, 23):
+        for n in (21, 22, 23):
             far_left(jnp.int32(n), (2,))
         for k in range(chunks):
             far_copy(3, place(jnp.int32(k))).wait_send()
@@ -650,7 +651,7 @@
             pltpu.VMEM((2, 2, 1, LANES), F32),
             pltpu.VMEM((2, nx, 1, LANES), F32),
             pltpu.VMEM((2, 2 * ny, 1, LANES), F32),
-            dma((7,)),
+            dma((8,)),
             dma((4, chunks)), dma((4, chunks)),
             dma((4, 2)), dma((4, chunks)),
             dma((4, 2)), dma((4, 2)),

time: 54.6 us -> 54.2 us (level)
  no operation moved by 1% of the time
where the time goes in v8:
time: 54.2 us; the launch traced here: 54.1 us
  Pallas kernels  51.7 us (95%)
  local copies, waits for them, and re-layouts  1.76 us (3%)
  between operations  0.64 us (1%)
    pallas_call x1, Pallas kernels, shards(): pl.pallas_call(functools.partial(kernel, (nx, ny, rows, cols)), out_shape...  51.7 us
    unnamed x2, local copies, waits for them, and re-layouts  1.76 us

profile of v8, /device:TPU:1, one launch (start us, length us, event | category | flops | bytes accessed | tf_op | source)
XLA Modules:
  0.0 54.1 jit_solution(11583063906654634821)
XLA Ops:
  0.6 51.7 %shard_map.86 = (f32[2,192,512]{2,1,0:T(8,128)S(1)}, f32[2,192,512]{2,1,0:T(8,128)S(1)}) custom-call(f32[192,512]{1,0:T(8,128)} %load_h.1, s32[192,512]{1,0:T(8,128)} %sink_h.1, s32[192,512]{1,0:T(8,128)} %pad_h.1, s32[2,192,512]{2,1,0:T(8,128)} %plane_h.1, s32[2,192,512]{2,1,0:T(8,128)} %via_h.1, f32[2,8]{1,0:T(2,128)} %plane_tab_h.1, f32[2,8]{1,0:T(2,128)} %via_tab_h.1), custom_call_target="tpu_custom_call" | custom-call | tf_op jit(solution)/shard_map/pallas_call | solution.py:667
  52.4 0.9 %copy.11 = f32[2,192,512]{2,1,0:T(8,128)} copy(f32[2,192,512]{2,1,0:T(8,128)S(1)} %get-tuple-element.2) | data formatting | bytes 1572864
  53.2 0.9 %copy.12 = f32[2,192,512]{2,1,0:T(8,128)} copy(f32[2,192,512]{2,1,0:T(8,128)S(1)} %get-tuple-element.3) | data formatting | bytes 1572864

commit v9 on v8

--- a/solution.py
+++ b/solution.py
@@ -38,7 +38,7 @@
 def kernel(
     sizes,
     load_h, sink_h, pad_h, plane_h, via_h, plane_tab_h, via_tab_h,
-    volt_ref, resid_ref,
+    volt_ref, resid_ref, step_ref,
     load_ref, sink_ref, pad_ref, plane_ref, via_ref, plane_tab, via_tab,
     via_mine, via_far,
     g_buf, g_e, g_w,
@@ -483,6 +483,7 @@
         line = line + got_p[0, 2 * k]
     mu, t00 = take(line, 0), take(line, 1)
     step, shift = mu / t00, t00 / mu
+    step_ref[...] = jnp.broadcast_to(step, (1, LANES))
 
     def third(a, b, c):
         return (b - step * c) - shift * (a - step * b)
@@ -577,7 +578,8 @@
     b2 = g2 - l2 - l3 * b1
     c2 = b2 / d2
     c1 = b1 / d1 - l3 * c2
-    c0 = step - l1 * c1 - l2 * c2
+    c0 = 1.0 - shift * (l1 * c1 + l2 * c2)
+    c1, c2 = shift * c1, shift * c2
 
     def finish(c, _):
         for slot in (0, 1):
@@ -588,7 +590,7 @@
                     c0 * p + c1 * (p - step * y1[slot, wide, :]) + c2 * z2[slot, wide, :]
                 )
                 tail = c0 * s1[slot, span, :] + c1 * s2[slot, span, :] + c2 * s3[slot, span, :]
-                resid_ref[layer[slot], span, :] = (src[span, :] - tail) if slot == 0 else -tail
+                resid_ref[layer[slot], span, :] = (shift * src[span, :] - tail) if slot == 0 else -tail
         return 0
 
     lax.fori_loop(0, chunks, finish, 0)
@@ -664,16 +666,17 @@
             pltpu.with_memory_space_constraint(a, pltpu.HBM)
             for a in (load_current, sink_mask, pad_mask, plane_class, via_class, plane_table, via_table)
         ]
-        return pl.pallas_call(
+        voltage, residual, step = pl.pallas_call(
             functools.partial(kernel, (nx, ny, rows, cols)),
-            out_shape=(shape, shape),
+            out_shape=(shape, shape, pltpu.VMEM((1, LANES), F32)),
             in_specs=[hbm] * 7,
-            out_specs=(vmem, vmem),
+            out_specs=(vmem, vmem, vmem),
             scratch_shapes=scratch,
             compiler_params=pltpu.CompilerParams(
                 collective_id=0, has_side_effects=True, vmem_limit_bytes=48 * 1024 * 1024
             ),
         )(*held)
+        return voltage * step[0, 0], residual * step[0, 0]
 
     layers = P("gz", "gy", "gx")
     plane = P("gy", "gx")

time: 54.2 us -> 53.8 us (level)
  local copies, waits for them, and re-layouts: 1.76 us -> 0 us
  other arithmetic: 0 us -> 1.33 us
    unnamed x2 -> x0, local copies, waits for them, and re-layouts: 1.76 us -> none
    mul x0 -> x1, other arithmetic: none -> 1.33 us  [shards(): return (voltage * step[0, 0], residual * step[0, 0])]
where the time goes in v9:
time: 53.8 us; the launch traced here: 53.7 us
  Pallas kernels  51.7 us (96%)
  other arithmetic  1.33 us (2%)
  between operations  0.64 us (1%)
    pallas_call x1, Pallas kernels, shards(): pl.pallas_call(functools.partial(kernel, (nx, ny, rows, cols)), out_shape...  51.7 us
    mul x1, other arithmetic, shards(): return (voltage * step[0, 0], residual * step[0, 0])  1.33 us

profile of v9, /device:TPU:1, one launch (start us, length us, event | category | flops | bytes accessed | tf_op | source)
XLA Modules:
  0.0 53.7 jit_solution(10468892687458892445)
XLA Ops:
  0.6 51.7 %shard_map.86 = (f32[2,192,512]{2,1,0:T(8,128)S(1)}, f32[2,192,512]{2,1,0:T(8,128)S(1)}, f32[1,128]{1,0:T(1,128)S(1)}) custom-call(f32[192,512]{1,0:T(8,128)} %load_h.1, s32[192,512]{1,0:T(8,128)} %sink_h.1, s32[192,512]{1,0:T(8,128)} %pad_h.1, s32[2,192,512]{2,1,0:T(8,128)} %plane_h.1, s32[2,192,512]{2,1,0:T(8,128)} %via_h.1, f32[2,8]{1,0:T(2,128)} %plane_tab_h.1, ...), custom_call_target="tpu_custom_call" | custom-call | tf_op jit(solution)/shard_map/pallas_call | solution.py:669
  52.4 1.3 %broadcast_multiply_fusion = (f32[2,192,512]{2,1,0:T(8,128)}, f32[2,192,512]{2,1,0:T(8,128)}) fusion(f32[2,192,512]{2,1,0:T(8,128)S(1)} %get-tuple-element.7, f32[]{:T(128)S(1)} %bitcast.2, f32[2,192,512]{2,1,0:T(8,128)S(1)} %get-tuple-element.5), kind=kLoop, calls=%fused_computation | loop fusion | flops 393216 | bytes 3145732 | tf_op jit(solution)/shard_map/mul | solution.py:679

commit v10 on v9

--- a/solution.py
+++ b/solution.py
@@ -561,13 +561,14 @@
     sums[5] = sums[5] - 2.0 * lax.cond(iz == 0, far_part, lambda: zero)
 
     line = line_of(sums)
-    for stage in (0, 1):
-        sum_start(1, stage, line)
-        line = sum_finish(1, stage)
+    sum_start(1, 0, line)
+    sum_start(1, 1, sum_finish(1, 0))
 
     @pl.when(iz == 1)
     def _():
         far_part()
+
+    line = sum_finish(1, 1)
 
     t01, t11, g1, t02, t12, t22, g2 = [take(line, k) / mu for k in range(7)]
     l1, l2 = t01 / shift, t02 / shift

time: 53.8 us -> 53.8 us (level)
  no operation moved by 1% of the time
where the time goes in v10:
time: 53.8 us; the launch traced here: 53.7 us
  Pallas kernels  51.7 us (96%)
  other arithmetic  1.33 us (2%)
  between operations  0.64 us (1%)
    pallas_call x1, Pallas kernels, shards(): pl.pallas_call(functools.partial(kernel, (nx, ny, rows, cols)), out_shape...  51.7 us
    mul x1, other arithmetic, shards(): return (voltage * step[0, 0], residual * step[0, 0])  1.33 us

profile of v10, /device:TPU:1, one launch (start us, length us, event | category | flops | bytes accessed | tf_op | source)
XLA Modules:
  0.0 53.7 jit_solution(3620062621261306893)
XLA Ops:
  0.6 51.7 %shard_map.86 = (f32[2,192,512]{2,1,0:T(8,128)S(1)}, f32[2,192,512]{2,1,0:T(8,128)S(1)}, f32[1,128]{1,0:T(1,128)S(1)}) custom-call(f32[192,512]{1,0:T(8,128)} %load_h.1, s32[192,512]{1,0:T(8,128)} %sink_h.1, s32[192,512]{1,0:T(8,128)} %pad_h.1, s32[2,192,512]{2,1,0:T(8,128)} %plane_h.1, s32[2,192,512]{2,1,0:T(8,128)} %via_h.1, f32[2,8]{1,0:T(2,128)} %plane_tab_h.1, ...), custom_call_target="tpu_custom_call" | custom-call | tf_op jit(solution)/shard_map/pallas_call | solution.py:670
  52.4 1.3 %broadcast_multiply_fusion = (f32[2,192,512]{2,1,0:T(8,128)}, f32[2,192,512]{2,1,0:T(8,128)}) fusion(f32[2,192,512]{2,1,0:T(8,128)S(1)} %get-tuple-element.7, f32[]{:T(128)S(1)} %bitcast.2, f32[2,192,512]{2,1,0:T(8,128)S(1)} %get-tuple-element.5), kind=kLoop, calls=%fused_computation | loop fusion | flops 393216 | bytes 3145732 | tf_op jit(solution)/shard_map/mul | solution.py:680
